TPU v7x, 128 devices: a whole 4x4x4 slice. The times are simulated.
128 devices in a mesh: dp: 1, b: 16 (over z, y), cp: 8 (over x, core).
Axes of the slice: x: 4, y: 4, z: 4, core: 2. Of those that a mesh axis runs over, the one named last changes fastest.
Arguments:
- x: bfloat16 [16, 2048, 2048], P(('dp', 'b'), 'cp')
- ids: int32 [16, 2048, 12], P(('dp', 'b'), 'cp')
- g_attn: bfloat16 [2048], replicated
- wq: bfloat16 [2048, 4096], replicated
- wk: bfloat16 [2048, 512], replicated
- wv: bfloat16 [2048, 512], replicated
- wo: bfloat16 [4096, 2048], replicated
- g_ffn: bfloat16 [2048], replicated
- w1: bfloat16 [2048, 6144], replicated
- w3: bfloat16 [2048, 6144], replicated
- w2: bfloat16 [6144, 2048], replicated
- g_moe: bfloat16 [2048], replicated
- wr: bfloat16 [2048, 192], replicated
- we_g: bfloat16 [128, 2048, 768], P(('b', 'cp'))
- we_u: bfloat16 [128, 2048, 768], P(('b', 'cp'))
- we_d: bfloat16 [128, 768, 2048], P(('b', 'cp'))
Outputs:
- output: bfloat16 [16, 2048, 2048], P(('dp', 'b'), 'cp')
All inputs are finite; a program needn't handle non-finite values.
Results may differ from a plain program's by a relative error of at most 0.00815073.
Values are sent between devices in bfloat16 or wider.
A program may use at most 1 GiB of HBM per device.

v0:
```python
import jax
import jax.numpy as jnp
from jax import lax
from jax.sharding import PartitionSpec as P

HEAD = 128
ROPE = 64
EPS = 1e-6
THETA = 10000.0
RSCALE = 2.5


def rms_norm(x, g):
    xf = x.astype(jnp.float32)
    r = lax.rsqrt(jnp.mean(xf * xf, axis=-1, keepdims=True) + EPS)
    return (xf * r * g.astype(jnp.float32)).astype(jnp.bfloat16)


def rope(t, pos):
    half = ROPE // 2
    freq = THETA ** (-jnp.arange(half, dtype=jnp.float32) / half)
    ang = pos.astype(jnp.float32)[:, None] * freq[None, :]
    c = jnp.cos(ang)[:, None, :]
    s = jnp.sin(ang)[:, None, :]
    tf = t.astype(jnp.float32)
    t1 = tf[..., :half]
    t2 = tf[..., half:ROPE]
    out = jnp.concatenate([t1 * c - t2 * s, t2 * c + t1 * s, tf[..., ROPE:]], axis=-1)
    return out.astype(jnp.bfloat16)


def proj(a, wt):
    return jnp.dot(a, wt, preferred_element_type=jnp.float32).astype(jnp.bfloat16)


def swiglu(z, wa, wb, wc):
    hh = (jax.nn.silu(jnp.dot(z, wa, preferred_element_type=jnp.float32)) * jnp.dot(z, wb, preferred_element_type=jnp.float32)).astype(jnp.bfloat16)
    return proj(hh, wc)


def attend(q, kb, vb, qpos, kpos, mx, den, acc):
    s = jnp.einsum('bkgqd,bskd->bkgqs', q, kb, preferred_element_type=jnp.float32) * (HEAD ** -0.5)
    s = jnp.where(qpos[:, None] >= kpos[None, :], s, -1e30)
    mnew = jnp.maximum(mx, jnp.max(s, axis=-1))
    corr = jnp.exp(mx - mnew)
    p = jnp.exp(s - mnew[..., None])
    den = den * corr + jnp.sum(p, axis=-1)
    pv = jnp.einsum('bkgqs,bskd->bkgqd', p.astype(jnp.bfloat16), vb, preferred_element_type=jnp.float32)
    acc = acc * corr[..., None] + pv
    return mnew, den, acc


def route(u, ids, wr, nexp):
    t = u.shape[0]
    top = ids.shape[-1]
    logits = jnp.dot(u, wr, preferred_element_type=jnp.float32)
    idf = ids.reshape(t, top)
    pick = idf[:, :, None] == jnp.arange(logits.shape[1])[None, None, :]
    gate = RSCALE * jax.nn.softmax(jnp.sum(jnp.where(pick, logits[:, None, :], 0.0), axis=-1), axis=-1)
    ffn = idf < nexp
    oh = pick[:, :, :nexp]
    cnt = jnp.sum(oh.astype(jnp.float32), axis=1)
    ti = jnp.arange(t)
    lower = (ti[None, :] < ti[:, None]).astype(jnp.bfloat16)
    excl = jnp.dot(lower, cnt.astype(jnp.bfloat16), preferred_element_type=jnp.float32)
    ji = jnp.arange(top)
    within = jnp.sum((idf[:, :, None] == idf[:, None, :]) & (ji[None, :] < ji[:, None])[None], axis=-1)
    rank = jnp.sum(jnp.where(oh, excl[:, None, :], 0.0), axis=-1).astype(jnp.int32) + within
    return gate, idf, ffn, rank, excl.T, (excl + cnt).T


def dispatch(u, first, last, cap):
    r = jnp.arange(cap, dtype=jnp.float32)[None, :, None]
    sel = ((r >= first[:, None, :]) & (r < last[:, None, :])).astype(jnp.bfloat16)
    return jnp.einsum('ect,td->ecd', sel, u, preferred_element_type=jnp.float32).astype(jnp.bfloat16)


def combine(got, gate, ffn, u):
    val = jnp.where(ffn[..., None], got.astype(jnp.float32), u.astype(jnp.float32)[:, None, :])
    return jnp.sum(gate[..., None] * val, axis=1)


def moe(u, ids, wr, we_g, we_u, we_d, ndev):
    t, d = u.shape
    top = ids.shape[-1]
    epd = we_g.shape[0]
    nexp = epd * ndev
    cap = t * top // nexp
    gate, idf, ffn, rank, first, last = route(u, ids, wr, nexp)
    idx = jnp.where(ffn, idf * cap + rank, 0)
    send = dispatch(u, first, last, cap).reshape(nexp * cap, d)
    recv = lax.all_to_all(send, ('b', 'cp'), 0, 0, tiled=True)
    xin = recv.reshape(ndev, epd, cap, d).transpose(1, 0, 2, 3).reshape(epd, ndev * cap, d)
    hg = jnp.einsum('ecd,edf->ecf', xin, we_g, preferred_element_type=jnp.float32)
    hu = jnp.einsum('ecd,edf->ecf', xin, we_u, preferred_element_type=jnp.float32)
    hh = (jax.nn.silu(hg) * hu).astype(jnp.bfloat16)
    yo = jnp.einsum('ecf,efd->ecd', hh, we_d, preferred_element_type=jnp.float32).astype(jnp.bfloat16)
    ret = yo.reshape(epd, ndev, cap, d).transpose(1, 0, 2, 3).reshape(nexp * cap, d)
    back = lax.all_to_all(ret, ('b', 'cp'), 0, 0, tiled=True)
    return combine(back[idx], gate, ffn, u)


def solution(mesh):
    ncp = mesh.shape['cp']
    ndev = mesh.shape['b'] * ncp
    tok = P(('dp', 'b'), 'cp', None)
    rep = P()
    exs = P(('b', 'cp'), None, None)

    def body(x, ids, g_attn, wq, wk, wv, wo, g_ffn, w1, w3, w2, g_moe, wr, we_g, we_u, we_d):
        bd, sd, d = x.shape
        nh = wq.shape[1] // HEAD
        kvh = wk.shape[1] // HEAD
        grp = nh // kvh
        ci = lax.axis_index('cp')
        pos = ci * sd + jnp.arange(sd)
        n = rms_norm(x, g_attn)
        q = rope(proj(n, wq).reshape(bd, sd, nh, HEAD), pos).reshape(bd, sd, kvh, grp, HEAD).transpose(0, 2, 3, 1, 4)
        kv = jnp.stack([rope(proj(n, wk).reshape(bd, sd, kvh, HEAD), pos), proj(n, wv).reshape(bd, sd, kvh, HEAD)])
        mx = jnp.full((bd, kvh, grp, sd), -1e30, jnp.float32)
        den = jnp.zeros((bd, kvh, grp, sd), jnp.float32)
        acc = jnp.zeros((bd, kvh, grp, sd, HEAD), jnp.float32)
        mx, den, acc = attend(q, kv[0], kv[1], pos, pos, mx, den, acc)
        perm = [(j, (j + 1) % ncp) for j in range(ncp)]
        for step in range(1, ncp):
            kv = lax.ppermute(kv, 'cp', perm)
            kpos = ((ci - step) % ncp) * sd + jnp.arange(sd)
            mx, den, acc = attend(q, kv[0], kv[1], pos, kpos, mx, den, acc)
        o = (acc / den[..., None]).astype(jnp.bfloat16).transpose(0, 3, 1, 2, 4).reshape(bd, sd, nh * HEAD)
        y = (x.astype(jnp.float32) + proj(o, wo).astype(jnp.float32)).astype(jnp.bfloat16)
        f = swiglu(rms_norm(y, g_ffn), w1, w3, w2)
        m = moe(rms_norm(x, g_moe).reshape(bd * sd, d), ids, wr, we_g, we_u, we_d, ndev)
        h = y.astype(jnp.float32) + f.astype(jnp.float32) + m.reshape(bd, sd, d)
        return h.astype(jnp.bfloat16)

    return jax.shard_map(body, mesh=mesh, in_specs=(tok, tok, rep, rep, rep, rep, rep, rep, rep, rep, rep, rep, rep, exs, exs, exs), out_specs=tok, check_vma=False)
```

profile of v0, /device:TPU:18, one launch (start us, length us, event | category | flops | bytes accessed | tf_op | source)
XLA Modules:
  0.0 654.0 jit_solution(10694547829082410028)
XLA Ops:
  33.5 20.9 %copy.145 = bf16[128,24,2048]{2,1,0:T(8,128)(2,1)} copy(bf16[128,24,2048]{2,0,1:T(8,128)(2,1)S(1)} %convolution_convert_fusion.1) | data formatting | bytes 25165824 | tf_op jit(solution)/shard_map/convert_element_type | solution.py:75
  54.4 12.3 %all-to-all-start = ((bf16[128,24,2048]{2,1,0:T(8,128)(2,1)}), bf16[128,24,2048]{2,1,0:T(8,128)(2,1)}, u32[]{:S(2)}, u32[]{:S(2)}) async-start(bf16[128,24,2048]{2,1,0:T(8,128)(2,1)} %copy.145), calls=%async_computation | async-start | bytes 25165824 | tf_op jit(solution)/shard_map/all_to_all | solution.py:92
  66.8 10.7 %fusion.100 = bf16[32,8,32,128]{3,1,2,0:T(8,128)(2,1)S(1)} fusion(bf16[2048,4096]{1,0:T(8,128)(2,1)} %param.19, bf16[1,256,2048]{2,1,0:T(8,128)(2,1)} %param.16, f32[2048]{0:T(1024)S(1)} %copy-done.76, f32[256]{0:T(256)S(1)} %copy-done.73), kind=kOutput, calls=%fused_computation.126 | convolution fusion | flops 4298113024 | bytes 19932160 | tf_op jit(solution)/shard_map/dot_general | solution.py:33
  98.2 130.6 %collective-permute-done.1 = bf16[2,1,256,4,128]{4,2,3,1,0:T(8,128)(2,1)} collective-permute-done((bf16[2,1,256,4,128]{4,2,3,1,0:T(8,128)(2,1)}, bf16[2,1,256,4,128]{4,2,3,1,0:T(8,128)(2,1)}, u32[]{:S(2)}, u32[]{:S(2)}) %collective-permute-start.1) | collective-permute-done | bytes 524320 | tf_op jit(solution)/shard_map/ppermute | solution.py:126
  228.8 6.1 maximum_bitcast_fusion
  243.7 6.5 collective-permute-done.3
  258.9 5.7 fusion.4
  292.3 5.9 fusion.15
  300.7 16.4 %fusion.77 = f32[3072,768]{1,0:T(8,128)} fusion(bf16[3072,2048]{1,0:T(8,128)(2,1)} %bitcast.64, bf16[1,2048,768]{2,1,0:T(8,128)(2,1)} %param.29), kind=kOutput, calls=%fused_computation.94 | convolution fusion | flops 9663676416 | bytes 25165824 | tf_op jit(solution)/shard_map/ecd,edf->ecf/dot_general | solution.py:94
  317.1 28.9 %convolution_convert_fusion = bf16[3072,2048]{1,0:T(8,128)(2,1)} fusion(f32[3072,768]{1,0:T(8,128)} %fusion.77, bf16[3072,2048]{1,0:T(8,128)(2,1)} %bitcast.64, bf16[1,768,2048]{2,1,0:T(8,128)(2,1)S(1)} %copy-done, bf16[1,2048,768]{2,1,0:T(8,128)(2,1)} %param.30), kind=kOutput, calls=%fused_computation.2 | convolution fusion | flops 19347800064 | bytes 40894464 | tf_op jit(solution)/shard_map/ecf,efd->ecd/dot_general | solution.py:97
  346.1 36.2 %all-to-all-start.1 = ((bf16[128,24,2048]{2,1,0:T(8,128)(2,1)}), bf16[128,24,2048]{2,1,0:T(8,128)(2,1)}, u32[]{:S(2)}, u32[]{:S(2)}) async-start(bf16[128,24,2048]{2,1,0:T(8,128)(2,1)} %bitcast.265), calls=%async_computation.1 | async-start | bytes 25165824 | tf_op jit(solution)/shard_map/all_to_all | solution.py:99
  387.5 5.3 fusion.21
  393.0 5.3 fusion.23
  403.3 5.3 fusion.37
  408.6 5.2 fusion.35
  413.8 7.7 %fusion.33 = f32[4,8,256,128]{2,3,1,0:T(8,128)} fusion(f32[4,8,256,256]{2,3,1,0:T(8,128)} %get-tuple-element.49, f32[4,8,256]{2,1,0:T(8,128)S(1)} %copy-done.42, pred[256,256]{0,1:T(8,128)(4,1)S(1)} %copy-done.17, bf16[2,1,256,4,128]{4,2,3,1,0:T(8,128)(2,1)} %collective-permute-done.2), kind=kOutput, calls=%fused_computation.52 | convolution fusion | flops 545259520 | bytes 12943360 | tf_op jit(solution)/shard_map/bkgqs,bskd->bkgqd/dot_general | solution.py:48
  434.0 13.2 %divide_convert_fusion = bf16[4,8,256,128]{2,3,1,0:T(8,128)(2,1)S(1)} fusion(f32[4,8,256,128]{2,3,1,0:T(8,128)} %fusion.27, f32[4,8,256,128]{2,3,1,0:T(8,128)} %fusion.29, f32[4,8,256,128]{2,3,1,0:T(8,128)} %fusion.31, f32[4,8,256,128]{2,3,1,0:T(8,128)} %fusion.33, f32[4,8,256,128]{2,3,1,0:T(8,128)} %fusion.35, f32[4,8,256,128]{2,3,1,0:T(8,128)} %fusion.37, ...), kind=kOutput, calls=%fused_computation.56 | convolution fusion | flops 563085312 | bytes 40501248 | tf_op jit(solution)/shard_map/bkgqs,bskd->bkgqd/dot_general | solution.py:48
  447.2 8.5 %fusion.95 = (f32[256]{0:T(256)S(1)}, bf16[1,256,2048]{2,1,0:T(8,128)(2,1)S(1)}) fusion(bf16[256,4096]{0,1:T(8,128)(2,1)S(1)} %bitcast.269, bf16[4096,2048]{1,0:T(8,128)(2,1)} %param.22, bf16[1,256,2048]{2,1,0:T(8,128)(2,1)S(1)} %copy-done.7), kind=kOutput, calls=%fused_computation.122 | convolution fusion | flops 4299161600 | bytes 20972544 | tf_op jit(solution)/shard_map/dot_general | solution.py:33
  456.8 14.5 %fusion.107 = f32[256,6144]{1,0:T(8,128)} fusion(bf16[2048,6144]{1,0:T(8,128)(2,1)} %param.24, bf16[1,256,2048]{2,1,0:T(8,128)(2,1)S(1)} %get-tuple-element.57, f32[2048]{0:T(1024)S(1)} %copy-done.77, f32[256]{0:T(256)S(1)} %add_rsqrt_fusion), kind=kOutput, calls=%fused_computation.135 | convolution fusion | flops 6444548096 | bytes 32515072 | tf_op jit(solution)/shard_map/dot_general | solution.py:37
  471.3 81.2 %all-to-all-done.1 = bf16[128,24,2048]{2,1,0:T(8,128)(2,1)} async-done(((bf16[128,24,2048]{2,1,0:T(8,128)(2,1)}), bf16[128,24,2048]{2,1,0:T(8,128)(2,1)}, u32[]{:S(2)}, u32[]{:S(2)}) %all-to-all-start.1) | async-done | bytes 12582944 | tf_op jit(solution)/shard_map/all_to_all | solution.py:99
  552.5 30.0 %gather_fusion = bf16[3072,2048]{1,0:T(8,128)(2,1)} fusion(bf16[3072,2048]{1,0:T(8,128)(2,1)} %bitcast.69, s32[3072]{0:T(1024)S(1)} %copy-done.15), kind=kCustom, calls=%fused_computation | custom fusion | bytes 25178112 | tf_op jit(solution)/shard_map/gather | solution.py:100
  582.5 21.8 %reshape.1104 = f32[256,12,2048]{2,1,0:T(8,128)} reshape(bf16[3072,2048]{1,0:T(8,128)(2,1)} %gather_fusion) | data formatting | bytes 37748736 | tf_op jit(solution)/shard_map/convert_element_type | solution.py:79
  604.3 19.3 %multiply_reduce_fusion = f32[256,2048]{1,0:T(8,128)} fusion(f32[256,12,2048]{2,1,0:T(8,128)} %reshape.1104, f32[256,2048]{1,0:T(8,128)S(1)} %copy-done.8, f32[256,12]{1,0:T(8,128)S(1)} %copy-done.47, pred[256,12]{1,0:T(8,128)(4,1)S(1)} %copy-done.60), kind=kLoop, calls=%fused_computation.1 | loop fusion | flops 18350080 | bytes 29375488 | tf_op jit(solution)/shard_map/reduce_sum | solution.py:80
  623.6 29.9 %fusion.91 = bf16[1,256,2048]{2,1,0:T(8,128)(2,1)} fusion(bf16[6144,2048]{1,0:T(8,128)(2,1)} %param.26, bf16[2048,6144]{1,0:T(8,128)(2,1)} %param.25, f32[256,6144]{1,0:T(8,128)} %fusion.107, bf16[1,256,2048]{2,1,0:T(8,128)(2,1)} %copy-done.30, f32[256,2048]{1,0:T(8,128)} %multiply_reduce_fusion, f32[2048]{0:T(1024)S(1)} %copy-done.77, ...), kind=kOutput, calls=%fused_computation.118 | convolution fusion | flops 12899581952 | bytes 60826624 | tf_op jit(solution)/shard_map/dot_general | solution.py:33
  (280 shorter events, 124.7 us)
Async XLA Ops:
  0.0 317.1 %copy-start = (bf16[1,768,2048]{2,1,0:T(8,128)(2,1)S(1)}, bf16[1,768,2048]{2,1,0:T(8,128)(2,1)}, u32[]{:S(2)}) copy-start(bf16[1,768,2048]{2,1,0:T(8,128)(2,1)} %param.31) | copy-start | bytes 9437188
  1.7 14.6 %copy-start.72 = (f32[256]{0:T(256)}, f32[256]{0:T(256)S(1)}, u32[]{:S(2)}) copy-start(f32[256]{0:T(256)S(1)} %add_rsqrt_fusion.1) | copy-start | bytes 3076
  7.9 15.2 %copy-start.61 = (s32[1,256,12]{1,0,2:T(1,128)S(1)}, s32[1,256,12]{1,0,2:T(1,128)}, u32[]{:S(2)}) copy-start(s32[1,256,12]{1,0,2:T(1,128)} %param.17) | copy-start | bytes 36868
  22.4 73.6 %collective-permute-start = (bf16[2,1,256,4,128]{4,2,3,1,0:T(8,128)(2,1)}, bf16[2,1,256,4,128]{4,2,3,1,0:T(8,128)(2,1)}, u32[]{:S(2)}, u32[]{:S(2)}) collective-permute-start(bf16[2,1,256,4,128]{4,2,3,1,0:T(8,128)(2,1)} %pad_maximum_fusion), channel_id=1, source_target_pairs={{0,1},{1,2},{2,3},{3,4},{4,5},{5,6},{6,7},{7,0},{8,9},{9,10},{10,1... | collective-permute-start | bytes 1572872 | tf_op jit(solution)/shard_map/ppermute | solution.py:126
  54.4 246.3 %all-to-all-start = ((bf16[128,24,2048]{2,1,0:T(8,128)(2,1)}), bf16[128,24,2048]{2,1,0:T(8,128)(2,1)}, u32[]{:S(2)}, u32[]{:S(2)}) async-start(bf16[128,24,2048]{2,1,0:T(8,128)(2,1)} %copy.145), calls=%async_computation | async-start | bytes 25165824 | tf_op jit(solution)/shard_map/all_to_all | solution.py:92
  93.3 141.6 %copy-start.79 = (bf16[2048]{0:T(1024)(128)(2,1)S(1)}, bf16[2048]{0:T(1024)(128)(2,1)}, u32[]{:S(2)}) copy-start(bf16[2048]{0:T(1024)(128)(2,1)} %param.23) | copy-start | bytes 12292
  96.0 132.8 %collective-permute-start.1 = (bf16[2,1,256,4,128]{4,2,3,1,0:T(8,128)(2,1)}, bf16[2,1,256,4,128]{4,2,3,1,0:T(8,128)(2,1)}, u32[]{:S(2)}, u32[]{:S(2)}) collective-permute-start(bf16[2,1,256,4,128]{4,2,3,1,0:T(8,128)(2,1)} %collective-permute-done), channel_id=1, source_target_pairs={{0,1},{1,2},{2,3},{3,4},{4,5},{5,6},{6,7},{7,0},{8,9},{9,10},{10,1... | collective-permute-start | bytes 1572872 | tf_op jit(solution)/shard_map/ppermute | solution.py:126
  228.8 12.9 %collective-permute-start.2 = (bf16[2,1,256,4,128]{4,2,3,1,0:T(8,128)(2,1)}, bf16[2,1,256,4,128]{4,2,3,1,0:T(8,128)(2,1)}, u32[]{:S(2)}, u32[]{:S(2)}) collective-permute-start(bf16[2,1,256,4,128]{4,2,3,1,0:T(8,128)(2,1)} %collective-permute-done.1), channel_id=1, source_target_pairs={{0,1},{1,2},{2,3},{3,4},{4,5},{5,6},{6,7},{7,0},{8,9},{9,10},{10,1... | collective-permute-start | bytes 1572872 | tf_op jit(solution)/shard_map/ppermute | solution.py:126
  241.1 43.1 %copy-start.50 = (f32[4,8,256]{2,1,0:T(8,128)}, f32[4,8,256]{2,1,0:T(8,128)S(1)}, u32[]{:S(2)}) copy-start(f32[4,8,256]{2,1,0:T(8,128)S(1)} %get-tuple-element.54) | copy-start | bytes 98308
  241.1 43.8 %copy-start.3 = (f32[4,8,256,256]{2,3,1,0:T(8,128)}, f32[4,8,256,256]{2,3,1,0:T(8,128)S(1)}, u32[]{:S(2)}) copy-start(f32[4,8,256,256]{2,3,1,0:T(8,128)S(1)} %get-tuple-element.55) | copy-start | bytes 25165828
  241.6 8.6 %collective-permute-start.3 = (bf16[2,1,256,4,128]{4,2,3,1,0:T(8,128)(2,1)}, bf16[2,1,256,4,128]{4,2,3,1,0:T(8,128)(2,1)S(1)}, u32[]{:S(2)}, u32[]{:S(2)}) collective-permute-start(bf16[2,1,256,4,128]{4,2,3,1,0:T(8,128)(2,1)} %collective-permute-done.2), channel_id=1, source_target_pairs={{0,1},{1,2},{2,3},{3,4},{4,5},{5,6},{6,7},{7,0},{8,9},{9,10},{10,1... | collective-permute-start | bytes 1572872 | tf_op jit(solution)/shard_map/ppermute | solution.py:126
  250.2 8.6 %collective-permute-start.4 = (bf16[2,1,256,4,128]{4,2,3,1,0:T(8,128)(2,1)S(1)}, bf16[2,1,256,4,128]{4,2,3,1,0:T(8,128)(2,1)S(1)}, u32[]{:S(2)}, u32[]{:S(2)}) collective-permute-start(bf16[2,1,256,4,128]{4,2,3,1,0:T(8,128)(2,1)S(1)} %collective-permute-done.3), channel_id=1, source_target_pairs={{0,1},{1,2},{2,3},{3,4},{4,5},{5,6},{6,7},{7,0},{8,9},{9,10},{10,1... | collective-permute-start | bytes 1572872 | tf_op jit(solution)/shard_map/ppermute | solution.py:126
  252.8 34.6 %copy-start.5 = (f32[4,8,256,256]{2,3,1,0:T(8,128)}, f32[4,8,256,256]{2,3,1,0:T(8,128)S(1)}, u32[]{:S(2)}) copy-start(f32[4,8,256,256]{2,3,1,0:T(8,128)S(1)} %get-tuple-element.53) | copy-start | bytes 25165828
  255.4 34.4 %copy-start.4 = (f32[4,8,256,256]{2,3,1,0:T(8,128)}, f32[4,8,256,256]{2,3,1,0:T(8,128)S(1)}, u32[]{:S(2)}) copy-start(f32[4,8,256,256]{2,3,1,0:T(8,128)S(1)} %get-tuple-element.51) | copy-start | bytes 25165828
  258.9 10.4 %collective-permute-start.5 = (bf16[2,1,256,4,128]{4,2,3,1,0:T(8,128)(2,1)S(1)}, bf16[2,1,256,4,128]{4,2,3,1,0:T(8,128)(2,1)S(1)}, u32[]{:S(2)}, u32[]{:S(2)}) collective-permute-start(bf16[2,1,256,4,128]{4,2,3,1,0:T(8,128)(2,1)S(1)} %collective-permute-done.4), channel_id=1, source_target_pairs={{0,1},{1,2},{2,3},{3,4},{4,5},{5,6},{6,7},{7,0},{8,9},{9,10},{10,1... | collective-permute-start | bytes 1572872 | tf_op jit(solution)/shard_map/ppermute | solution.py:126
  269.3 10.2 %collective-permute-start.6 = (bf16[2,1,256,4,128]{4,2,3,1,0:T(8,128)(2,1)S(1)}, bf16[2,1,256,4,128]{4,2,3,1,0:T(8,128)(2,1)S(1)}, u32[]{:S(2)}, u32[]{:S(2)}) collective-permute-start(bf16[2,1,256,4,128]{4,2,3,1,0:T(8,128)(2,1)S(1)} %collective-permute-done.5), channel_id=1, source_target_pairs={{0,1},{1,2},{2,3},{3,4},{4,5},{5,6},{6,7},{7,0},{8,9},{9,10},{10,1... | collective-permute-start | bytes 1572872 | tf_op jit(solution)/shard_map/ppermute | solution.py:126
  346.1 36.2 %copy-start.38 = (f32[4,8,256]{2,1,0:T(8,128)S(1)}, f32[4,8,256]{2,1,0:T(8,128)}, u32[]{:S(2)}) copy-start(f32[4,8,256]{2,1,0:T(8,128)} %get-tuple-element.15) | copy-start | bytes 98308
  346.1 206.4 %all-to-all-start.1 = ((bf16[128,24,2048]{2,1,0:T(8,128)(2,1)}), bf16[128,24,2048]{2,1,0:T(8,128)(2,1)}, u32[]{:S(2)}, u32[]{:S(2)}) async-start(bf16[128,24,2048]{2,1,0:T(8,128)(2,1)} %bitcast.265), calls=%async_computation.1 | async-start | bytes 25165824 | tf_op jit(solution)/shard_map/all_to_all | solution.py:99
  387.5 15.8 %slice-start.4 = ((s8[8388608]{0:T(1024)(128)(4,1)}), s8[4194304]{0:T(1024)(128)(4,1)S(1)}, s32[]{:S(2)}) async-start(s8[8388608]{0:T(1024)(128)(4,1)} %bitcast.253), calls=%async_computation.6 | async-start | bytes 8388608
  456.8 95.7 %copy-start.15 = (s32[3072]{0:T(1024)S(1)}, s32[3072]{0:T(1024)}, u32[]{:S(2)}) copy-start(s32[3072]{0:T(1024)} %broadcast_clamp_fusion) | copy-start | bytes 36868
  582.5 21.8 %copy-start.8 = (f32[256,2048]{1,0:T(8,128)S(1)}, f32[256,2048]{1,0:T(8,128)}, u32[]{:S(2)}) copy-start(f32[256,2048]{1,0:T(8,128)} %bitcast_convert_fusion) | copy-start | bytes 6291460
  582.5 21.8 %copy-start.47 = (f32[256,12]{1,0:T(8,128)S(1)}, f32[256,12]{1,0:T(8,128)}, u32[]{:S(2)}) copy-start(f32[256,12]{1,0:T(8,128)} %copy.141) | copy-start | bytes 36868
  582.5 21.8 %copy-start.60 = (pred[256,12]{1,0:T(8,128)(4,1)S(1)}, pred[256,12]{1,0:T(8,128)(4,1)}, u32[]{:S(2)}) copy-start(pred[256,12]{1,0:T(8,128)(4,1)} %copy.142) | copy-start | bytes 9220
  623.6 29.9 %copy-start.1 = (bf16[1,768,2048]{2,1,0:T(8,128)(2,1)S(1)}, bf16[1,768,2048]{2,1,0:T(8,128)(2,1)}, u32[]{:S(2)}) copy-start(bf16[1,768,2048]{2,1,0:T(8,128)(2,1)} %param.31) | copy-start | bytes 9437188
  (79 other events, 499.2 us)
where the time goes:
time: 667 us; the launch traced here: 654 us
  waiting for transfers between devices  222 us (33%)
  matrix products  205 us (31%)
  local copies, waits for them, and re-layouts  97.3 us (15%)
  other arithmetic  78.7 us (12%)
  starting transfers between devices  49.3 us (7%)
    ppermute x7, waiting for transfers between devices, body(): kv = lax.ppermute(kv, 'cp', perm)  141 us
    all_to_all x1, waiting for transfers between devices, moe(): back = lax.all_to_all(ret, ('b', 'cp'), 0, 0, tiled=True)  81.2 us
    dot_general x5, matrix products, proj(): jnp.dot(a, wt, preferred_element_type=jnp.float32).astype(jnp.bfloat16)  56 us
    dot_general x8, matrix products, attend(): jnp.einsum('bkgqs,bskd->bkgqd', p.astype(jnp.bfloat16), vb, preferred_ele...  47.7 us
    all_to_all x1, starting transfers between devices, moe(): back = lax.all_to_all(ret, ('b', 'cp'), 0, 0, tiled=True)  36.2 us
    dot_general x8, matrix products, attend(): jnp.einsum('bkgqd,bskd->bkgqs', q, kb, preferred_element_type=jnp.float32)  33.1 us
    reduce_sum x8, other arithmetic, attend(): den = den * corr + jnp.sum(p, axis=-1)  31.6 us
    gather x1, local copies, waits for them, and re-layouts, moe(): return combine(back[idx], gate, ffn, u)  30 us
  transfers between devices with their start and end apart: 9, of which 5 were waited for; matrix products, arithmetic and copies ran while one was open for 32% of the time, Pallas kernels for 0%

commit v1 on v0

v1 whole, which is shorter than its diff:
```python
import functools

import jax
import jax.numpy as jnp
from jax import lax
from jax.experimental import pallas as pl
from jax.experimental.pallas import tpu as pltpu
from jax.sharding import PartitionSpec as P

HEAD = 128
ROPE = 64
EPS = 1e-6
THETA = 10000.0
RSCALE = 2.5
LOG2E = 1.4426950408889634
F32 = jnp.float32
BF16 = jnp.bfloat16


def rms_norm(x, g):
    xf = x.astype(F32)
    r = lax.rsqrt(jnp.mean(xf * xf, axis=-1, keepdims=True) + EPS)
    return (xf * r * g.astype(F32)).astype(BF16)


def proj(a, wt):
    return jnp.dot(a, wt, preferred_element_type=F32).astype(BF16)


def rope_tables(pos):
    half = ROPE // 2
    freq = THETA ** (-jnp.arange(half, dtype=F32) / half)
    ang = pos.astype(F32)[:, None] * freq[None, :]
    c, s = jnp.cos(ang), jnp.sin(ang)
    rest = jnp.ones((pos.shape[0], HEAD - ROPE), F32)
    return jnp.concatenate([c, c, rest], axis=-1), jnp.concatenate([-s, s, 0.0 * rest], axis=-1)


def rotate(t, c, s):
    half = ROPE // 2
    lane = lax.broadcasted_iota(jnp.int32, t.shape, 1)
    partner = jnp.where(lane < half, pltpu.roll(t, HEAD - half, 1), pltpu.roll(t, half, 1))
    return (t * c + partner * s).astype(BF16)


def vmem(n):
    return [pl.BlockSpec(memory_space=pltpu.VMEM)] * n


def front_kernel(x_ref, ids_ref, ga_ref, gm_ref, wk_ref, wv_ref, wr_ref, c_ref, s_ref, n_ref, u_ref, kv_ref, gate_ref, zero_ref, ex_ref, ext_ref):
    t, d = x_ref.shape
    nexp = ex_ref.shape[1]
    xf = x_ref[...].astype(F32)
    xr = xf * lax.rsqrt(jnp.mean(xf * xf, axis=-1, keepdims=True) + EPS)
    n = (xr * ga_ref[...].astype(F32)).astype(BF16)
    u = (xr * gm_ref[...].astype(F32)).astype(BF16)
    n_ref[...] = n
    u_ref[...] = u
    kd = wk_ref.shape[1]
    k = jnp.dot(n, wk_ref[...], preferred_element_type=F32).astype(BF16).astype(F32)
    for i in range(kd // HEAD):
        kv_ref[:, i * HEAD:(i + 1) * HEAD] = rotate(k[:, i * HEAD:(i + 1) * HEAD], c_ref[...], s_ref[...])
    kv_ref[:, kd:] = jnp.dot(n, wv_ref[...], preferred_element_type=F32).astype(BF16)
    logits = jnp.dot(u, wr_ref[...], preferred_element_type=F32)
    col = lax.broadcasted_iota(jnp.int32, logits.shape, 1)
    ids = ids_ref[...]
    mult = jnp.zeros(logits.shape, F32)
    for j in range(ids.shape[1]):
        mult += (ids[:, j:j + 1] == col).astype(F32)
    has = mult > 0.0
    top = jnp.max(jnp.where(has, logits, -jnp.inf), axis=-1, keepdims=True)
    e = jnp.where(has, mult * jnp.exp(jnp.minimum(logits - top, 0.0)), 0.0)
    gate = RSCALE * e / jnp.sum(e, axis=-1, keepdims=True)
    zero = jnp.sum(jnp.where(col >= nexp, gate, 0.0), axis=-1, keepdims=True)
    zero_ref[...] = jnp.broadcast_to(zero, zero_ref.shape)
    g = gate[:, :nexp]
    for i in range(3):
        part = g.astype(BF16)
        gate_ref[i * t:(i + 1) * t, :] = part
        g = g - part.astype(F32)
    here = has[:, :nexp]
    ti = lax.broadcasted_iota(jnp.int32, (t, t), 0)
    tj = lax.broadcasted_iota(jnp.int32, (t, t), 1)
    before = jnp.where(tj < ti, 1.0, 0.0).astype(BF16)
    rank = jnp.dot(before, jnp.where(here, 1.0, 0.0).astype(BF16), preferred_element_type=F32)
    rank = jnp.where(here, rank, -1.0)
    ex_ref[...] = rank.astype(BF16)
    ext_ref[...] = rank.T.astype(BF16)


def front(x, ids, ga, gm, wk, wv, wr, c, s, nexp):
    t, d = x.shape
    kd = wk.shape[1]
    shapes = [((t, d), BF16), ((t, d), BF16), ((t, 2 * kd), BF16), ((3 * t, nexp), BF16), ((t, HEAD), F32), ((t, nexp), BF16), ((nexp, t), BF16)]
    return pl.pallas_call(
        front_kernel,
        out_shape=[jax.ShapeDtypeStruct(*a) for a in shapes],
        in_specs=vmem(9),
        out_specs=vmem(7),
        cost_estimate=pl.CostEstimate(flops=2 * t * d * (2 * kd + wr.shape[1]), bytes_accessed=8 << 20, transcendentals=0),
        compiler_params=pltpu.CompilerParams(vmem_limit_bytes=48 << 20),
        name="front",
    )(x, ids, ga.reshape(1, d), gm.reshape(1, d), wk, wv, wr, c, s)


def dispatch_kernel(cap, ext_ref, u_ref, o_ref):
    rows = o_ref.shape[0]
    nexp = ext_ref.shape[0]
    r = pl.program_id(0) * rows + lax.broadcasted_iota(jnp.int32, (rows, nexp), 0)
    lo = cap * lax.broadcasted_iota(jnp.int32, (rows, nexp), 1)
    own = (r >= lo) & (r < lo + cap)
    rank = jnp.dot(jnp.where(own, 1.0, 0.0).astype(BF16), ext_ref[...], preferred_element_type=F32)
    slot = jnp.sum(jnp.where(own, (r - lo).astype(F32), 0.0), axis=-1, keepdims=True)
    sel = jnp.where(rank == slot, 1.0, 0.0).astype(BF16)
    o_ref[...] = jnp.dot(sel, u_ref[...], preferred_element_type=F32).astype(BF16)


def dispatch(ext, u, cap):
    nexp, t = ext.shape
    d = u.shape[1]
    rows = 16 * cap
    return pl.pallas_call(
        functools.partial(dispatch_kernel, cap),
        grid=(nexp * cap // rows,),
        out_shape=jax.ShapeDtypeStruct((nexp * cap, d), BF16),
        in_specs=[pl.BlockSpec((nexp, t), lambda i: (0, 0)), pl.BlockSpec((t, d), lambda i: (0, 0))],
        out_specs=pl.BlockSpec((rows, d), lambda i: (i, 0)),
        cost_estimate=pl.CostEstimate(flops=2 * nexp * cap * t * d, bytes_accessed=nexp * cap * d * 2, transcendentals=0),
        name="dispatch",
    )(ext, u)


def attend_kernel(grp, ci_ref, q_ref, k_ref, v_ref, c_ref, s_ref, o_ref, sc_ref):
    sd = q_ref.shape[0]
    ci = ci_ref[0]
    row = lax.broadcasted_iota(jnp.int32, (sd, sd), 0)
    colm = lax.broadcasted_iota(jnp.int32, (sd, sd), 1)
    for h in range(q_ref.shape[1] // HEAD):
        q = rotate(q_ref[:, h * HEAD:(h + 1) * HEAD].astype(F32), c_ref[...], s_ref[...])

        def score(j):
            kb = k_ref[pl.ds(pl.multiple_of(j * sd, sd), sd), :]
            return lax.dot_general(q, kb, (((1,), (1,)), ((), ())), preferred_element_type=F32) * (HEAD ** -0.5 * LOG2E)

        def fold(a, op):
            r = a[:, :HEAD]
            for i in range(1, sd // HEAD):
                r = op(r, a[:, i * HEAD:(i + 1) * HEAD])
            return r

        def first(j, m):
            sc = score(j)
            sc_ref[j] = sc
            return jnp.maximum(m, fold(sc, jnp.maximum))

        last = jnp.where(row >= colm, score(ci), -1e30)
        mx = lax.fori_loop(0, ci, first, fold(last, jnp.maximum))
        mx = jnp.max(mx, axis=-1, keepdims=True)

        def weigh(sc, j, den, acc):
            p = jnp.exp2(sc - mx)
            vb = v_ref[pl.ds(pl.multiple_of(j * sd, sd), sd), :]
            return den + fold(p, jnp.add), acc + jnp.dot(p.astype(BF16), vb, preferred_element_type=F32)

        zero = jnp.zeros((sd, HEAD), F32)
        den, acc = weigh(last, ci, zero, zero)
        den, acc = lax.fori_loop(0, ci, lambda j, st: weigh(sc_ref[j], j, *st), (den, acc))
        o_ref[:, h * HEAD:(h + 1) * HEAD] = (acc / jnp.sum(den, axis=-1, keepdims=True)).astype(BF16)


def attention(ci, q, kv, c, s, ncp):
    sd, qd = q.shape
    kvh = kv.shape[1] // (2 * HEAD)
    nh = qd // HEAD
    grp = nh // kvh
    per = 4 if grp % 4 == 0 else 1
    steps = nh // per
    ga = grp // per
    return pl.pallas_call(
        functools.partial(attend_kernel, grp),
        grid_spec=pltpu.PrefetchScalarGridSpec(
            num_scalar_prefetch=1,
            grid=(steps,),
            in_specs=[
                pl.BlockSpec((sd, per * HEAD), lambda i, ci: (0, i)),
                pl.BlockSpec((kv.shape[0], HEAD), lambda i, ci: (0, i // ga)),
                pl.BlockSpec((kv.shape[0], HEAD), lambda i, ci: (0, kvh + i // ga)),
                pl.BlockSpec((sd, HEAD), lambda i, ci: (0, 0)),
                pl.BlockSpec((sd, HEAD), lambda i, ci: (0, 0)),
            ],
            out_specs=pl.BlockSpec((sd, per * HEAD), lambda i, ci: (0, i)),
            scratch_shapes=[pltpu.VMEM((ncp, sd, sd), F32)],
        ),
        out_shape=jax.ShapeDtypeStruct((sd, qd), BF16),
        cost_estimate=pl.CostEstimate(flops=16 * sd * kv.shape[0] * qd, bytes_accessed=8 << 20, transcendentals=0),
        name="attention",
    )(ci, q, kv, kv, c, s)


def combine_kernel(cap, back_ref, gate_ref, ex_ref, zero_ref, u_ref, y_ref, f_ref, h_ref, acc_ref):
    rows = back_ref.shape[0]
    t, nexp = ex_ref.shape
    r = pl.program_id(0) * rows + lax.broadcasted_iota(jnp.int32, (nexp, rows), 1)
    lo = cap * lax.broadcasted_iota(jnp.int32, (nexp, rows), 0)
    own = (r >= lo) & (r < lo + cap)
    spread = jnp.where(own, 1.0, 0.0).astype(BF16)
    slot = jnp.sum(jnp.where(own, (r - lo).astype(F32), 0.0), axis=0, keepdims=True)
    hit = jnp.dot(ex_ref[...], spread, preferred_element_type=F32) == slot
    back = back_ref[...]

    @pl.when(pl.program_id(0) == 0)
    def _():
        acc_ref[...] = zero_ref[:, :1] * u_ref[...].astype(F32)

    tot = None
    for i in range(3):
        w = jnp.dot(gate_ref[i * t:(i + 1) * t, :], spread, preferred_element_type=F32)
        p = jnp.dot(jnp.where(hit, w, 0.0).astype(BF16), back, preferred_element_type=F32)
        tot = p if tot is None else tot + p
    acc_ref[...] += tot

    @pl.when(pl.program_id(0) == pl.num_programs(0) - 1)
    def _():
        h_ref[...] = (y_ref[...].astype(F32) + f_ref[...].astype(F32) + acc_ref[...]).astype(BF16)


def combine(back, gate, ex, zero, u, y, f, cap):
    t, d = u.shape
    nexp = ex.shape[1]
    rows = 16 * cap
    whole = lambda a: pl.BlockSpec(a.shape, lambda i: (0, 0))
    return pl.pallas_call(
        functools.partial(combine_kernel, cap),
        grid=(nexp * cap // rows,),
        out_shape=jax.ShapeDtypeStruct((t, d), BF16),
        in_specs=[pl.BlockSpec((rows, d), lambda i: (i, 0))] + [whole(a) for a in (gate, ex, zero, u, y, f)],
        out_specs=pl.BlockSpec((t, d), lambda i: (0, 0)),
        scratch_shapes=[pltpu.VMEM((t, d), F32)],
        cost_estimate=pl.CostEstimate(flops=6 * nexp * cap * t * d, bytes_accessed=nexp * cap * d * 2, transcendentals=0),
        name="combine",
    )(back, gate, ex, zero, u, y, f)


def solution(mesh):
    ncp = mesh.shape['cp']
    ndev = mesh.shape['b'] * ncp
    tok = P(('dp', 'b'), 'cp', None)
    rep = P()
    exs = P(('b', 'cp'), None, None)
    axes = ('b', 'cp')

    def body(x, ids, g_attn, wq, wk, wv, wo, g_ffn, w1, w3, w2, g_moe, wr, we_g, we_u, we_d):
        bd, sd, d = x.shape
        top = ids.shape[-1]
        x = x.reshape(sd, d)
        ids = ids.reshape(sd, top)
        cap = sd * top // ndev
        ci = lax.axis_index('cp')

        c, s = rope_tables(ci * sd + jnp.arange(sd))
        n, u, kv, gate, zero, ex, ext = front(x, ids, g_attn, g_moe, wk, wv, wr, c, s, ndev)
        kv = lax.all_gather(kv, 'cp', axis=0, tiled=True)
        send = dispatch(ext, u, cap)
        recv = lax.all_to_all(send, axes, 0, 0, tiled=True)

        q = proj(n, wq)
        o = attention(ci.reshape(1), q, kv, c, s, ncp)
        y = (x.astype(F32) + proj(o, wo).astype(F32)).astype(BF16)
        z = rms_norm(y, g_ffn)
        hid = (jax.nn.silu(jnp.dot(z, w1, preferred_element_type=F32)) * jnp.dot(z, w3, preferred_element_type=F32)).astype(BF16)
        f = proj(hid, w2)

        eh = (jax.nn.silu(jnp.dot(recv, we_g[0], preferred_element_type=F32)) * jnp.dot(recv, we_u[0], preferred_element_type=F32)).astype(BF16)
        out = proj(eh, we_d[0])
        back = lax.all_to_all(out, axes, 0, 0, tiled=True)
        h = combine(back, gate, ex, zero, u, y, f, cap)
        return h.reshape(bd, sd, d)

    return jax.shard_map(body, mesh=mesh, in_specs=(tok, tok, rep, rep, rep, rep, rep, rep, rep, rep, rep, rep, rep, exs, exs, exs), out_specs=tok, check_vma=False)
```

time: 667 us -> 490 us (0.73)
  the two profiles are of different devices: /device:TPU:18 before, /device:TPU:98 now
where the time goes in v1:
time: 490 us; the launch traced here: 489 us
  waiting for transfers between devices  254 us (52%)
  matrix products  105 us (21%)
  Pallas kernels  82.3 us (17%)
  starting transfers between devices  21.3 us (4%)
  between operations  13.5 us (3%)
  local copies, waits for them, and re-layouts  12.6 us (3%)
    all_to_all x1, waiting for transfers between devices, body(): recv = lax.all_to_all(send, axes, 0, 0, tiled=True)  181 us
    dot_general x4, matrix products, proj(): return jnp.dot(a, wt, preferred_element_type=F32).astype(BF16)  74.2 us
    all_to_all x1, waiting for transfers between devices, body(): back = lax.all_to_all(out, axes, 0, 0, tiled=True)  72.8 us
    pallas_call x1, Pallas kernels, attention(): pl.pallas_call(functools.partial(attend_kernel, grp), grid_spec=pltpu.Pre...  44.6 us
    pallas_call x1, Pallas kernels, combine(): pl.pallas_call(functools.partial(combine_kernel, cap), grid=(nexp * cap /...  23.7 us
    dot_general x1, matrix products, body(): jnp.dot(recv, we_g[0], preferred_element_type=F32)  16 us
    dot_general x1, matrix products, body(): jnp.dot(z, w1, preferred_element_type=F32)  14.8 us
    unnamed x36, local copies, waits for them, and re-layouts  11 us
  transfers between devices with their start and end apart: 3, of which 2 were waited for; matrix products, arithmetic and copies ran while one was open for 21% of the time, Pallas kernels for 9%

profile of v1, /device:TPU:98, one launch (start us, length us, event | category | flops | bytes accessed | tf_op | source)
XLA Modules:
  0.0 489.2 jit_solution(15967332425484000752)
XLA Ops:
  6.6 1.0 copy.19
  7.5 0.7 reshape.44.ga_ref
  8.2 0.7 reshape.45.gm_ref
  8.9 2.2 copy.21.wr_ref
  12.0 1.3 copy-done.2
  13.3 1.2 copy-done.3
  14.5 4.6 front.1
  19.1 0.9 copy-done.5
  20.1 0.8 copy-done.8
  21.5 1.0 copy-done.10
  22.4 0.7 copy-done.12
  24.4 9.5 %dispatch.1 = bf16[3072,2048]{1,0:T(8,128)(2,1)} custom-call(bf16[128,256]{1,0:T(8,128)(2,1)} %copy-done.9, bf16[256,2048]{1,0:T(8,128)(2,1)} %copy-done.5), custom_call_target="tpu_custom_call" | custom-call | flops 3221225472 | bytes 12582912 | tf_op jit(solution)/shard_map/dispatch/pallas_call | solution.py:122
  33.9 10.2 %all-to-all-start = ((bf16[128,24,2048]{2,1,0:T(8,128)(2,1)}), bf16[128,24,2048]{2,1,0:T(8,128)(2,1)}, u32[]{:S(2)}, u32[]{:S(2)}) async-start(bf16[128,24,2048]{2,1,0:T(8,128)(2,1)} %bitcast.30), calls=%async_computation | async-start | bytes 25165824 | tf_op jit(solution)/shard_map/all_to_all | solution.py:264
  44.9 180.5 %all-to-all-done = bf16[128,24,2048]{2,1,0:T(8,128)(2,1)} async-done(((bf16[128,24,2048]{2,1,0:T(8,128)(2,1)}), bf16[128,24,2048]{2,1,0:T(8,128)(2,1)}, u32[]{:S(2)}, u32[]{:S(2)}) %all-to-all-start) | async-done | bytes 12582944 | tf_op jit(solution)/shard_map/all_to_all | solution.py:264
  225.4 16.0 %fusion.5 = f32[3072,768]{1,0:T(8,128)} fusion(bf16[3072,2048]{1,0:T(8,128)(2,1)} %bitcast.3, bf16[1,2048,768]{2,1,0:T(8,128)(2,1)} %param.29), kind=kOutput, calls=%fused_computation.8 | convolution fusion | flops 9663676416 | bytes 25165824 | tf_op jit(solution)/shard_map/dot_general | solution.py:273
  241.4 28.9 %convolution_convert_fusion = bf16[3072,2048]{1,0:T(8,128)(2,1)} fusion(f32[3072,768]{1,0:T(8,128)} %fusion.5, bf16[3072,2048]{1,0:T(8,128)(2,1)} %bitcast.3, bf16[1,768,2048]{2,1,0:T(8,128)(2,1)S(1)} %copy-done, bf16[1,2048,768]{2,1,0:T(8,128)(2,1)} %param.30), kind=kOutput, calls=%fused_computation | convolution fusion | flops 19347800064 | bytes 40894464 | tf_op jit(solution)/shard_map/dot_general | solution.py:27
  270.4 10.8 %all-to-all-start.1 = ((bf16[128,24,2048]{2,1,0:T(8,128)(2,1)}), bf16[128,24,2048]{2,1,0:T(8,128)(2,1)}, u32[]{:S(2)}, u32[]{:S(2)}) async-start(bf16[128,24,2048]{2,1,0:T(8,128)(2,1)} %bitcast.31), calls=%async_computation.1 | async-start | bytes 25165824 | tf_op jit(solution)/shard_map/all_to_all | solution.py:275
  281.2 11.5 %convolution_convert_fusion.1.q_ref = bf16[256,4096]{1,0:T(8,128)(2,1)} fusion(bf16[256,2048]{1,0:T(8,128)(2,1)S(1)} %copy-done.11, bf16[2048,4096]{1,0:T(8,128)(2,1)} %param.19), kind=kOutput, calls=%fused_computation.4 | convolution fusion | flops 4296015872 | bytes 19922944 | tf_op jit(solution)/shard_map/dot_general | solution.py:27
  292.7 44.6 %attention.1 = bf16[256,4096]{1,0:T(8,128)(2,1)} custom-call(s32[1]{0:T(128)} %bitcast.9.ci_ref, bf16[256,4096]{1,0:T(8,128)(2,1)} %convolution_convert_fusion.1.q_ref, bf16[2048,1024]{1,0:T(8,128)(2,1)} %all-gather.2.cloned.1.call-done.k_ref.v_ref, bf16[2048,1024]{1,0:T(8,128)(2,1)} %all-gather.2.cloned.1.call-done.k_ref.v_ref, f32[256,128]{1,0:T(8,128)} %copy-done.6, ...), custom_call_target="tpu_custom_call" | custom-call | flops 34359738368 | bytes 8388608 | tf_op jit(solution)/shard_map/attention/pallas_call | solution.py:179
  337.3 11.0 %fusion.12 = (f32[256]{0:T(256)S(1)}, bf16[256,2048]{1,0:T(8,128)(2,1)S(1)}) fusion(bf16[256,4096]{1,0:T(8,128)(2,1)} %attention.1, bf16[4096,2048]{1,0:T(8,128)(2,1)} %param.22, bf16[1,256,2048]{2,1,0:T(8,128)(2,1)S(1)} %copy-done.4), kind=kOutput, calls=%fused_computation.18 | convolution fusion | flops 4299161600 | bytes 20972544 | tf_op jit(solution)/shard_map/dot_general | solution.py:27
  348.3 14.8 %fusion.17 = f32[256,6144]{1,0:T(8,128)} fusion(bf16[2048,6144]{1,0:T(8,128)(2,1)} %param.24, bf16[256,2048]{1,0:T(8,128)(2,1)S(1)} %get-tuple-element.23.y_ref, f32[2048]{0:T(1024)S(1)} %convert_element_type.52, f32[256]{0:T(256)S(1)} %add_rsqrt_fusion), kind=kOutput, calls=%fused_computation.21 | convolution fusion | flops 6444548096 | bytes 32515072 | tf_op jit(solution)/shard_map/dot_general | solution.py:270
  363.1 22.7 %fusion.11.f_ref = bf16[256,2048]{1,0:T(8,128)(2,1)} fusion(bf16[6144,2048]{1,0:T(8,128)(2,1)} %param.26, bf16[2048,6144]{1,0:T(8,128)(2,1)} %param.25, f32[256,6144]{1,0:T(8,128)} %fusion.17, bf16[256,2048]{1,0:T(8,128)(2,1)S(1)} %get-tuple-element.23.y_ref, f32[2048]{0:T(1024)S(1)} %convert_element_type.52, f32[256]{0:T(256)S(1)} %add_rsqrt_fusion), kind=kOutput, calls=%fused_computation.17 | convolution fusion | flops 12896960512 | bytes 58729472 | tf_op jit(solution)/shard_map/dot_general | solution.py:27
  385.9 72.8 %all-to-all-done.1 = bf16[128,24,2048]{2,1,0:T(8,128)(2,1)} async-done(((bf16[128,24,2048]{2,1,0:T(8,128)(2,1)}), bf16[128,24,2048]{2,1,0:T(8,128)(2,1)}, u32[]{:S(2)}, u32[]{:S(2)}) %all-to-all-start.1) | async-done | bytes 12582944 | tf_op jit(solution)/shard_map/all_to_all | solution.py:275
  458.7 23.7 %combine.1 = bf16[256,2048]{1,0:T(8,128)(2,1)} custom-call(bf16[3072,2048]{1,0:T(8,128)(2,1)} %bitcast.8.back_ref, bf16[768,128]{1,0:T(8,128)(2,1)} %copy-done.12, bf16[256,128]{1,0:T(8,128)(2,1)} %copy-done.14, f32[256,128]{1,0:T(8,128)} %copy-done.13, bf16[256,2048]{1,0:T(8,128)(2,1)} %copy-done.5, bf16[256,2048]{1,0:T(8,128)(2,1)} %copy-done.16, ...), custom_call_target="tpu_custom_call" | custom-call | flops 9663676416 | bytes 12582912 | tf_op jit(solution)/shard_map/combine/pallas_call | solution.py:232
  (41 shorter events, 3.5 us)
Async XLA Ops:
  6.5 234.9 %copy-start = (bf16[1,768,2048]{2,1,0:T(8,128)(2,1)S(1)}, bf16[1,768,2048]{2,1,0:T(8,128)(2,1)}, u32[]{:S(2)}) copy-start(bf16[1,768,2048]{2,1,0:T(8,128)(2,1)} %param.31) | copy-start | bytes 9437188
  12.0 21.9 %copy-start.6 = (f32[256,128]{1,0:T(8,128)}, f32[256,128]{1,0:T(8,128)S(1)}, u32[]{:S(2)}) copy-start(f32[256,128]{1,0:T(8,128)S(1)} %get-tuple-element.24.c_ref) | copy-start | bytes 393220
  12.0 21.9 %copy-start.7 = (f32[256,128]{1,0:T(8,128)}, f32[256,128]{1,0:T(8,128)S(1)}, u32[]{:S(2)}) copy-start(f32[256,128]{1,0:T(8,128)S(1)} %get-tuple-element.25.s_ref) | copy-start | bytes 393220
  12.0 1.3 copy-start.2
  13.3 1.2 copy-start.3
  19.1 1.0 copy-start.5
  20.1 0.8 copy-start.8
  20.9 0.6 copy-start.9
  21.5 1.0 copy-start.10
  22.4 0.7 copy-start.12
  23.1 0.6 copy-start.13
  23.8 0.6 copy-start.14
  33.9 11.0 %copy-start.15 = (bf16[2048]{0:T(1024)(128)(2,1)S(1)}, bf16[2048]{0:T(1024)(128)(2,1)}, u32[]{:S(2)}) copy-start(bf16[2048]{0:T(1024)(128)(2,1)} %param.23) | copy-start | bytes 12292
  33.9 191.6 %all-to-all-start = ((bf16[128,24,2048]{2,1,0:T(8,128)(2,1)}), bf16[128,24,2048]{2,1,0:T(8,128)(2,1)}, u32[]{:S(2)}, u32[]{:S(2)}) async-start(bf16[128,24,2048]{2,1,0:T(8,128)(2,1)} %bitcast.30), calls=%async_computation | async-start | bytes 25165824 | tf_op jit(solution)/shard_map/all_to_all | solution.py:264
  44.1 248.5 %all-gather.2.cloned.1.call-start = ((), (), s32[]{:S(2)}) async-start(), calls=%async_computation.2 | async-start | bytes 4718592 | tf_op jit(solution)/shard_map/all_gather | solution.py:262
  270.4 10.8 %copy-start.11 = (bf16[256,2048]{1,0:T(8,128)(2,1)S(1)}, bf16[256,2048]{1,0:T(8,128)(2,1)}, u32[]{:S(2)}) copy-start(bf16[256,2048]{1,0:T(8,128)(2,1)} %copy-done.10) | copy-start | bytes 3145732
  270.4 188.3 %all-to-all-start.1 = ((bf16[128,24,2048]{2,1,0:T(8,128)(2,1)}), bf16[128,24,2048]{2,1,0:T(8,128)(2,1)}, u32[]{:S(2)}, u32[]{:S(2)}) async-start(bf16[128,24,2048]{2,1,0:T(8,128)(2,1)} %bitcast.31), calls=%async_computation.1 | async-start | bytes 25165824 | tf_op jit(solution)/shard_map/all_to_all | solution.py:275
  292.7 44.6 %copy-start.4 = (bf16[1,256,2048]{2,1,0:T(8,128)(2,1)S(1)}, bf16[1,256,2048]{2,1,0:T(8,128)(2,1)}, u32[]{:S(2)}) copy-start(bf16[1,256,2048]{2,1,0:T(8,128)(2,1)} %param.16) | copy-start | bytes 3145732
  348.3 14.8 %copy-start.16 = (bf16[256,2048]{1,0:T(8,128)(2,1)}, bf16[256,2048]{1,0:T(8,128)(2,1)S(1)}, u32[]{:S(2)}) copy-start(bf16[256,2048]{1,0:T(8,128)(2,1)S(1)} %get-tuple-element.23.y_ref) | copy-start | bytes 3145732
  458.7 23.7 %copy-start.1 = (bf16[1,768,2048]{2,1,0:T(8,128)(2,1)S(1)}, bf16[1,768,2048]{2,1,0:T(8,128)(2,1)}, u32[]{:S(2)}) copy-start(bf16[1,768,2048]{2,1,0:T(8,128)(2,1)} %param.31) | copy-start | bytes 9437188
Sparse Core Ops, SparseCore 0:
  46.7 55.5 all-gather.1

commit v2 on v1

--- a/solution.py
+++ b/solution.py
@@ -197,53 +197,161 @@
     )(ci, q, kv, kv, c, s)
 
 
-def combine_kernel(cap, back_ref, gate_ref, ex_ref, zero_ref, u_ref, y_ref, f_ref, h_ref, acc_ref):
-    rows = back_ref.shape[0]
+def expert_kernel(cap, nb, ncp, ny, recv, wg, wu, wd, gate_ref, ex_ref, zero_ref, u_ref, y_ref, f_ref, h_ref, made, back, ibuf, obuf, bbuf, acc_ref, isem, osem, bsem, ssem, rsem):
+    b, c = lax.axis_index('b'), lax.axis_index('cp')
+    nz = nb // ny
+    me = b * ncp + c
+    rows = ncp * cap
     t, nexp = ex_ref.shape
-    r = pl.program_id(0) * rows + lax.broadcasted_iota(jnp.int32, (nexp, rows), 1)
-    lo = cap * lax.broadcasted_iota(jnp.int32, (nexp, rows), 0)
-    own = (r >= lo) & (r < lo + cap)
-    spread = jnp.where(own, 1.0, 0.0).astype(BF16)
-    slot = jnp.sum(jnp.where(own, (r - lo).astype(F32), 0.0), axis=0, keepdims=True)
-    hit = jnp.dot(ex_ref[...], spread, preferred_element_type=F32) == slot
-    back = back_ref[...]
-
-    @pl.when(pl.program_id(0) == 0)
-    def _():
-        acc_ref[...] = zero_ref[:, :1] * u_ref[...].astype(F32)
-
-    tot = None
-    for i in range(3):
-        w = jnp.dot(gate_ref[i * t:(i + 1) * t, :], spread, preferred_element_type=F32)
-        p = jnp.dot(jnp.where(hit, w, 0.0).astype(BF16), back, preferred_element_type=F32)
-        tot = p if tot is None else tot + p
-    acc_ref[...] += tot
-
-    @pl.when(pl.program_id(0) == pl.num_programs(0) - 1)
-    def _():
-        h_ref[...] = (y_ref[...].astype(F32) + f_ref[...].astype(F32) + acc_ref[...]).astype(BF16)
-
-
-def combine(back, gate, ex, zero, u, y, f, cap):
+
+    def shifted(k, sign):
+        dy, dz = k % ny, k // ny
+        return (b // ny + sign * dz + nz) % nz * ny + (b % ny + sign * dy + ny) % ny
+
+    def block(ref, g):
+        return ref.at[pl.ds(pl.multiple_of(g * rows, rows), rows)]
+
+    def chunk(ref, e):
+        return ref.at[pl.ds(pl.multiple_of(e * cap, cap), cap)]
+
+    def load(k):
+        return pltpu.make_async_copy(block(recv, shifted(k, 1)), ibuf.at[k % 2], isem.at[k % 2])
+
+    def store(k):
+        return pltpu.make_async_copy(obuf.at[k % 2], block(made, shifted(k, 1)), osem.at[k % 2])
+
+    def give(g, p):
+        return pltpu.make_async_remote_copy(
+            src_ref=chunk(made, g * ncp + p), dst_ref=chunk(back, me), send_sem=ssem.at[g * ncp + p], recv_sem=rsem.at[me],
+            device_id={'b': g, 'cp': p}, device_id_type=pl.DeviceIdType.MESH)
+
+    def keep():
+        return pltpu.make_async_copy(chunk(made, me), chunk(back, me), rsem.at[me])
+
+    def send(k):
+        g = shifted(k, 1)
+
+        def one(i, _):
+            give(g, (c + i) % ncp).start()
+            return 0
+
+        @pl.when(k == 0)
+        def _():
+            keep().start()
+
+        lax.fori_loop(jnp.where(k == 0, 1, 0), ncp, one, 0)
+
+    load(0).start()
+
+    def work(k, _):
+        load(k).wait()
+
+        @pl.when(k + 1 < nb)
+        def _():
+            load(k + 1).start()
+
+        x = ibuf[k % 2]
+        a = jnp.dot(x, wg[...], preferred_element_type=F32)
+        hid = (a * (1.0 / (1.0 + jnp.exp(-a))) * jnp.dot(x, wu[...], preferred_element_type=F32)).astype(BF16)
+
+        @pl.when(k > 0)
+        def _():
+            store(k - 1).wait()
+            send(k - 1)
+
+        obuf[k % 2] = jnp.dot(hid, wd[...], preferred_element_type=F32).astype(BF16)
+        store(k).start()
+        return 0
+
+    lax.fori_loop(0, nb, work, 0)
+    store(nb - 1).wait()
+    send(nb - 1)
+
+    acc_ref[...] = zero_ref[:, :1] * u_ref[...].astype(F32)
+
+    def fetch(k):
+        return pltpu.make_async_copy(block(back, shifted(k, -1)), bbuf.at[k % 2], bsem.at[k % 2])
+
+    def arrive(k):
+        g = shifted(k, -1)
+
+        def one(i, _):
+            pltpu.make_async_copy(chunk(back, g * ncp + i), chunk(back, g * ncp + i), rsem.at[g * ncp + i]).wait()
+            return 0
+
+        lax.fori_loop(0, ncp, one, 0)
+        fetch(k).start()
+
+    def add(k, _):
+        @pl.when(k < nb)
+        def _():
+            arrive(k)
+
+        @pl.when(k > 0)
+        def _():
+            kk = k - 1
+            fetch(kk).wait()
+            r = shifted(kk, -1) * rows + lax.broadcasted_iota(jnp.int32, (nexp, rows), 1)
+            lo = cap * lax.broadcasted_iota(jnp.int32, (nexp, rows), 0)
+            own = (r >= lo) & (r < lo + cap)
+            spread = jnp.where(own, 1.0, 0.0).astype(BF16)
+            slot = jnp.sum(jnp.where(own, (r - lo).astype(F32), 0.0), axis=0, keepdims=True)
+            hit = jnp.dot(ex_ref[...], spread, preferred_element_type=F32) == slot
+            got = bbuf[kk % 2]
+            tot = acc_ref[...]
+            for i in range(3):
+                w = jnp.dot(gate_ref[i * t:(i + 1) * t, :], spread, preferred_element_type=F32)
+                tot += jnp.dot(jnp.where(hit, w, 0.0).astype(BF16), got, preferred_element_type=F32)
+            acc_ref[...] = tot
+
+        return 0
+
+    lax.fori_loop(0, nb + 1, add, 0)
+    h_ref[...] = (y_ref[...].astype(F32) + f_ref[...].astype(F32) + acc_ref[...]).astype(BF16)
+
+    def drain(k, _):
+        g = shifted(k, 1)
+
+        def one(i, _):
+            give(g, (c + i) % ncp).wait_send()
+            return 0
+
+        lax.fori_loop(jnp.where(k == 0, 1, 0), ncp, one, 0)
+        return 0
+
+    lax.fori_loop(0, nb, drain, 0)
+
+
+def experts(recv, wg, wu, wd, gate, ex, zero, u, y, f, cap, nb, ncp, ny):
     t, d = u.shape
-    nexp = ex.shape[1]
-    rows = 16 * cap
-    whole = lambda a: pl.BlockSpec(a.shape, lambda i: (0, 0))
+    n, rows = nb * ncp, ncp * cap
+    hbm = pl.BlockSpec(memory_space=pl.ANY)
     return pl.pallas_call(
-        functools.partial(combine_kernel, cap),
-        grid=(nexp * cap // rows,),
-        out_shape=jax.ShapeDtypeStruct((t, d), BF16),
-        in_specs=[pl.BlockSpec((rows, d), lambda i: (i, 0))] + [whole(a) for a in (gate, ex, zero, u, y, f)],
-        out_specs=pl.BlockSpec((t, d), lambda i: (0, 0)),
-        scratch_shapes=[pltpu.VMEM((t, d), F32)],
-        cost_estimate=pl.CostEstimate(flops=6 * nexp * cap * t * d, bytes_accessed=nexp * cap * d * 2, transcendentals=0),
-        name="combine",
-    )(back, gate, ex, zero, u, y, f)
+        functools.partial(expert_kernel, cap, nb, ncp, ny),
+        out_shape=[jax.ShapeDtypeStruct(a, BF16) for a in ((t, d), recv.shape, recv.shape)],
+        in_specs=[hbm] + vmem(9),
+        out_specs=vmem(1) + [hbm, hbm],
+        scratch_shapes=[
+            pltpu.VMEM((2, rows, d), BF16),
+            pltpu.VMEM((2, rows, d), BF16),
+            pltpu.VMEM((2, rows, d), BF16),
+            pltpu.VMEM((t, d), F32),
+            pltpu.SemaphoreType.DMA((2,)),
+            pltpu.SemaphoreType.DMA((2,)),
+            pltpu.SemaphoreType.DMA((2,)),
+            pltpu.SemaphoreType.DMA((n,)),
+            pltpu.SemaphoreType.DMA((n,)),
+        ],
+        cost_estimate=pl.CostEstimate(flops=100 << 30, bytes_accessed=32 << 20, transcendentals=0),
+        compiler_params=pltpu.CompilerParams(vmem_limit_bytes=56 << 20, has_side_effects=True),
+        name="experts",
+    )(recv, wg, wu, wd, gate, ex, zero, u, y, f)[0]
 
 
 def solution(mesh):
     ncp = mesh.shape['cp']
     ndev = mesh.shape['b'] * ncp
+    ny = 4 if mesh.shape['b'] % 4 == 0 else 1
     tok = P(('dp', 'b'), 'cp', None)
     rep = P()
     exs = P(('b', 'cp'), None, None)
@@ -260,7 +368,7 @@
         c, s = rope_tables(ci * sd + jnp.arange(sd))
         n, u, kv, gate, zero, ex, ext = front(x, ids, g_attn, g_moe, wk, wv, wr, c, s, ndev)
         kv = lax.all_gather(kv, 'cp', axis=0, tiled=True)
-        send = dispatch(ext, u, cap)
+        send, kv = lax.optimization_barrier((dispatch(ext, u, cap), kv))
         recv = lax.all_to_all(send, axes, 0, 0, tiled=True)
 
         q = proj(n, wq)
@@ -270,10 +378,7 @@
         hid = (jax.nn.silu(jnp.dot(z, w1, preferred_element_type=F32)) * jnp.dot(z, w3, preferred_element_type=F32)).astype(BF16)
         f = proj(hid, w2)
 
-        eh = (jax.nn.silu(jnp.dot(recv, we_g[0], preferred_element_type=F32)) * jnp.dot(recv, we_u[0], preferred_element_type=F32)).astype(BF16)
-        out = proj(eh, we_d[0])
-        back = lax.all_to_all(out, axes, 0, 0, tiled=True)
-        h = combine(back, gate, ex, zero, u, y, f, cap)
+        h = experts(recv, we_g[0], we_u[0], we_d[0], gate, ex, zero, u, y, f, cap, ndev // ncp, ncp, ny)
         return h.reshape(bd, sd, d)
 
     return jax.shard_map(body, mesh=mesh, in_specs=(tok, tok, rep, rep, rep, rep, rep, rep, rep, rep, rep, rep, rep, exs, exs, exs), out_specs=tok, check_vma=False)

time: 490 us -> 509 us (1.039)
  the two profiles are of different devices: /device:TPU:98 before, /device:TPU:41 now
where the time goes in v2:
time: 509 us; the launch traced here: 508 us
  Pallas kernels  308 us (61%)
  waiting for transfers between devices  106 us (21%)
  matrix products  60.1 us (12%)
  between operations  13.5 us (3%)
  local copies, waits for them, and re-layouts  11 us (2%)
  starting transfers between devices  8.52 us (2%)
    pallas_call x1, Pallas kernels, experts(): pl.pallas_call(functools.partial(expert_kernel, cap, nb, ncp, ny), out_sh...  261 us
    all_to_all x1, waiting for transfers between devices, body(): recv = lax.all_to_all(send, axes, 0, 0, tiled=True)  81.4 us
    dot_general x3, matrix products, proj(): return jnp.dot(a, wt, preferred_element_type=F32).astype(BF16)  45.3 us
    pallas_call x1, Pallas kernels, attention(): pl.pallas_call(functools.partial(attend_kernel, grp), grid_spec=pltpu.Pre...  32.3 us
    all_gather x1, waiting for transfers between devices, body(): kv = lax.all_gather(kv, 'cp', axis=0, tiled=True)  24.8 us
    dot_general x1, matrix products, body(): jnp.dot(z, w1, preferred_element_type=F32)  14.8 us
  transfers between devices with their start and end apart: 2, of which 2 were waited for; matrix products, arithmetic and copies ran while one was open for 12% of the time, Pallas kernels for 8%

profile of v2, /device:TPU:41, one launch (start us, length us, event | category | flops | bytes accessed | tf_op | source)
XLA Modules:
  0.0 508.2 jit_solution(1452093402819833095)
XLA Ops:
  6.7 0.7 reshape.42.ga_ref
  7.4 0.7 reshape.43.gm_ref
  8.1 0.8 copy.19
  8.9 1.4 copy.21.wr_ref
  10.4 0.5 fusion.14
  10.9 0.1 maximum_maximum_fusion
  11.1 1.3 copy-done
  12.4 5.1 front.1
  17.5 1.0 copy-done.2
  18.4 0.6 copy-done.5
  19.1 0.7 copy-done.6
  19.7 0.6 copy-done.7
  20.4 0.6 copy-done.8
  21.1 9.5 %dispatch.1 = bf16[3072,2048]{1,0:T(8,128)(2,1)} custom-call(bf16[128,256]{1,0:T(8,128)(2,1)} %copy-done.5, bf16[256,2048]{1,0:T(8,128)(2,1)} %copy-done.2), custom_call_target="tpu_custom_call" | custom-call | flops 3221225472 | bytes 12582912 | tf_op jit(solution)/shard_map/dispatch/pallas_call | solution.py:122
  30.5 24.8 %all-gather.2.cloned.1.call-done.k_ref.v_ref = bf16[2048,1024]{1,0:T(8,128)(2,1)} async-done(((bf16[256,1024]{1,0:T(8,128)(2,1)}), bf16[2048,1024]{1,0:T(8,128)(2,1)}) %all-gather.2.cloned.1.call-update) | async-done | bytes 4194320 | tf_op jit(solution)/shard_map/all_gather | solution.py:370
  55.3 8.5 %all-to-all-start = ((bf16[128,24,2048]{2,1,0:T(8,128)(2,1)}), bf16[128,24,2048]{2,1,0:T(8,128)(2,1)}, u32[]{:S(2)}, u32[]{:S(2)}) async-start(bf16[128,24,2048]{2,1,0:T(8,128)(2,1)} %bitcast.19), calls=%async_computation | async-start | bytes 25165824 | tf_op jit(solution)/shard_map/all_to_all | solution.py:372
  63.8 11.5 %convolution_convert_fusion.q_ref = bf16[256,4096]{1,0:T(8,128)(2,1)} fusion(bf16[256,2048]{1,0:T(8,128)(2,1)S(1)} %get-tuple-element.22, bf16[2048,4096]{1,0:T(8,128)(2,1)} %param.19), kind=kOutput, calls=%fused_computation.2 | convolution fusion | flops 4296015872 | bytes 19922944 | tf_op jit(solution)/shard_map/dot_general | solution.py:27
  75.3 32.3 %attention.1 = bf16[256,4096]{1,0:T(8,128)(2,1)} custom-call(s32[1]{0:T(128)} %bitcast.7.ci_ref, bf16[256,4096]{1,0:T(8,128)(2,1)} %convolution_convert_fusion.q_ref, bf16[2048,1024]{1,0:T(8,128)(2,1)} %all-gather.2.cloned.1.call-done.k_ref.v_ref, bf16[2048,1024]{1,0:T(8,128)(2,1)} %all-gather.2.cloned.1.call-done.k_ref.v_ref, f32[256,128]{1,0:T(8,128)} %copy-done.3, ...), custom_call_target="tpu_custom_call" | custom-call | flops 34359738368 | bytes 8388608 | tf_op jit(solution)/shard_map/attention/pallas_call | solution.py:179
  107.6 11.1 %fusion.7 = (f32[256]{0:T(256)S(1)}, bf16[256,2048]{1,0:T(8,128)(2,1)S(1)}) fusion(bf16[256,4096]{1,0:T(8,128)(2,1)} %attention.1, bf16[4096,2048]{1,0:T(8,128)(2,1)} %param.22, bf16[1,256,2048]{2,1,0:T(8,128)(2,1)S(1)} %copy-done.1), kind=kOutput, calls=%fused_computation.12 | convolution fusion | flops 4299161600 | bytes 20972544 | tf_op jit(solution)/shard_map/dot_general | solution.py:27
  118.7 14.8 %fusion.12 = f32[256,6144]{1,0:T(8,128)} fusion(bf16[2048,6144]{1,0:T(8,128)(2,1)} %param.24, bf16[256,2048]{1,0:T(8,128)(2,1)S(1)} %get-tuple-element.29.y_ref, f32[2048]{0:T(1024)S(1)} %convert_element_type.44, f32[256]{0:T(256)S(1)} %add_rsqrt_fusion), kind=kOutput, calls=%fused_computation.15 | convolution fusion | flops 6444548096 | bytes 32515072 | tf_op jit(solution)/shard_map/dot_general | solution.py:378
  133.5 22.8 %fusion.6.f_ref = bf16[256,2048]{1,0:T(8,128)(2,1)} fusion(bf16[6144,2048]{1,0:T(8,128)(2,1)} %param.26, bf16[2048,6144]{1,0:T(8,128)(2,1)} %param.25, f32[256,6144]{1,0:T(8,128)} %fusion.12, bf16[256,2048]{1,0:T(8,128)(2,1)S(1)} %get-tuple-element.29.y_ref, f32[2048]{0:T(1024)S(1)} %convert_element_type.44, f32[256]{0:T(256)S(1)} %add_rsqrt_fusion), kind=kOutput, calls=%fused_computation.11 | convolution fusion | flops 12896960512 | bytes 58729472 | tf_op jit(solution)/shard_map/dot_general | solution.py:27
  156.3 81.4 %all-to-all-done = bf16[128,24,2048]{2,1,0:T(8,128)(2,1)} async-done(((bf16[128,24,2048]{2,1,0:T(8,128)(2,1)}), bf16[128,24,2048]{2,1,0:T(8,128)(2,1)}, u32[]{:S(2)}, u32[]{:S(2)}) %all-to-all-start) | async-done | bytes 12582944 | tf_op jit(solution)/shard_map/all_to_all | solution.py:372
  237.7 261.3 %experts.1 = (bf16[256,2048]{1,0:T(8,128)(2,1)}, bf16[3072,2048]{1,0:T(8,128)(2,1)}, bf16[3072,2048]{1,0:T(8,128)(2,1)}) custom-call(bf16[3072,2048]{1,0:T(8,128)(2,1)} %bitcast.3.recv, bf16[2048,768]{1,0:T(8,128)(2,1)} %bitcast.21, bf16[2048,768]{1,0:T(8,128)(2,1)} %bitcast.22, bf16[768,2048]{1,0:T(8,128)(2,1)} %bitcast.23, bf16[768,128]{1,0:T(8,128)(2,1)} %copy-done.6, ...), custom_call_target="tpu_custom_call" | custom-call | flops 107374182400 | bytes 33554432 | tf_op jit(solution)/shard_map/experts/pallas_call | solution.py:329
  499.1 2.3 copy.23
  (26 shorter events, 0.2 us)
Async XLA Ops:
  6.5 14.5 %copy-start.9 = (bf16[2048]{0:T(1024)(128)(2,1)S(1)}, bf16[2048]{0:T(1024)(128)(2,1)}, u32[]{:S(2)}) copy-start(bf16[2048]{0:T(1024)(128)(2,1)} %param.23) | copy-start | bytes 12292
  6.5 48.8 %all-gather.2.cloned.1.call-start = ((), (), s32[]{:S(2)}) async-start(), calls=%async_computation.1 | async-start | bytes 4718592 | tf_op jit(solution)/shard_map/all_gather | solution.py:370
  11.1 19.5 %copy-start.3 = (f32[256,128]{1,0:T(8,128)}, f32[256,128]{1,0:T(8,128)S(1)}, u32[]{:S(2)}) copy-start(f32[256,128]{1,0:T(8,128)S(1)} %get-tuple-element.30.c_ref) | copy-start | bytes 393220
  11.1 19.5 %copy-start.4 = (f32[256,128]{1,0:T(8,128)}, f32[256,128]{1,0:T(8,128)S(1)}, u32[]{:S(2)}) copy-start(f32[256,128]{1,0:T(8,128)S(1)} %get-tuple-element.31.s_ref) | copy-start | bytes 393220
  11.1 1.3 copy-start
  17.5 1.0 copy-start.2
  18.4 0.6 copy-start.5
  19.1 0.7 copy-start.6
  19.7 0.6 copy-start.7
  20.4 0.6 copy-start.8
  55.3 182.4 %all-to-all-start = ((bf16[128,24,2048]{2,1,0:T(8,128)(2,1)}), bf16[128,24,2048]{2,1,0:T(8,128)(2,1)}, u32[]{:S(2)}, u32[]{:S(2)}) async-start(bf16[128,24,2048]{2,1,0:T(8,128)(2,1)} %bitcast.19), calls=%async_computation | async-start | bytes 25165824 | tf_op jit(solution)/shard_map/all_to_all | solution.py:372
  75.3 32.3 %copy-start.1 = (bf16[1,256,2048]{2,1,0:T(8,128)(2,1)S(1)}, bf16[1,256,2048]{2,1,0:T(8,128)(2,1)}, u32[]{:S(2)}) copy-start(bf16[1,256,2048]{2,1,0:T(8,128)(2,1)} %param.16) | copy-start | bytes 3145732
  118.7 14.8 %copy-start.10 = (bf16[256,2048]{1,0:T(8,128)(2,1)}, bf16[256,2048]{1,0:T(8,128)(2,1)S(1)}, u32[]{:S(2)}) copy-start(bf16[256,2048]{1,0:T(8,128)(2,1)S(1)} %get-tuple-element.29.y_ref) | copy-start | bytes 3145732
Sparse Core Ops, SparseCore 0:
  21.2 34.0 all-gather.1

commit v3 on v1

--- a/solution.py
+++ b/solution.py
@@ -12,6 +12,7 @@
 EPS = 1e-6
 THETA = 10000.0
 RSCALE = 2.5
+PARTS = 2
 LOG2E = 1.4426950408889634
 F32 = jnp.float32
 BF16 = jnp.bfloat16
@@ -130,42 +131,50 @@
     )(ext, u)
 
 
-def attend_kernel(grp, ci_ref, q_ref, k_ref, v_ref, c_ref, s_ref, o_ref, sc_ref):
+def attend_kernel(per, ci_ref, q_ref, k_ref, v_ref, c_ref, s_ref, o_ref, q_all, sc_ref, mx_ref, den_ref, acc_ref):
     sd = q_ref.shape[0]
     ci = ci_ref[0]
-    row = lax.broadcasted_iota(jnp.int32, (sd, sd), 0)
-    colm = lax.broadcasted_iota(jnp.int32, (sd, sd), 1)
-    for h in range(q_ref.shape[1] // HEAD):
-        q = rotate(q_ref[:, h * HEAD:(h + 1) * HEAD].astype(F32), c_ref[...], s_ref[...])
-
-        def score(j):
-            kb = k_ref[pl.ds(pl.multiple_of(j * sd, sd), sd), :]
-            return lax.dot_general(q, kb, (((1,), (1,)), ((), ())), preferred_element_type=F32) * (HEAD ** -0.5 * LOG2E)
-
-        def fold(a, op):
-            r = a[:, :HEAD]
-            for i in range(1, sd // HEAD):
-                r = op(r, a[:, i * HEAD:(i + 1) * HEAD])
-            return r
-
-        def first(j, m):
-            sc = score(j)
-            sc_ref[j] = sc
-            return jnp.maximum(m, fold(sc, jnp.maximum))
-
-        last = jnp.where(row >= colm, score(ci), -1e30)
-        mx = lax.fori_loop(0, ci, first, fold(last, jnp.maximum))
-        mx = jnp.max(mx, axis=-1, keepdims=True)
-
-        def weigh(sc, j, den, acc):
-            p = jnp.exp2(sc - mx)
-            vb = v_ref[pl.ds(pl.multiple_of(j * sd, sd), sd), :]
-            return den + fold(p, jnp.add), acc + jnp.dot(p.astype(BF16), vb, preferred_element_type=F32)
-
-        zero = jnp.zeros((sd, HEAD), F32)
-        den, acc = weigh(last, ci, zero, zero)
-        den, acc = lax.fori_loop(0, ci, lambda j, st: weigh(sc_ref[j], j, *st), (den, acc))
-        o_ref[:, h * HEAD:(h + 1) * HEAD] = (acc / jnp.sum(den, axis=-1, keepdims=True)).astype(BF16)
+    for h in range(per):
+        q_all[h * sd:(h + 1) * sd, :] = rotate(q_ref[:, h * HEAD:(h + 1) * HEAD].astype(F32), c_ref[...], s_ref[...])
+
+    def fold(a, op):
+        r = a[:, :HEAD]
+        for i in range(1, sd // HEAD):
+            r = op(r, a[:, i * HEAD:(i + 1) * HEAD])
+        return r
+
+    def score(j):
+        kb = k_ref[pl.ds(pl.multiple_of(j * sd, sd), sd), :]
+        return lax.dot_general(q_all[...], kb, (((1,), (1,)), ((), ())), preferred_element_type=F32) * (HEAD ** -0.5 * LOG2E)
+
+    row = lax.broadcasted_iota(jnp.int32, (per * sd, sd), 0) % sd
+    last = jnp.where(row >= lax.broadcasted_iota(jnp.int32, (per * sd, sd), 1), score(ci), -1e30)
+    sc_ref[ci] = last
+    mx_ref[...] = fold(last, jnp.maximum)
+
+    def first(j, _):
+        sc = score(j)
+        sc_ref[j] = sc
+        mx_ref[...] = jnp.maximum(mx_ref[...], fold(sc, jnp.maximum))
+        return 0
+
+    lax.fori_loop(0, ci, first, 0)
+    mx_ref[...] = jnp.broadcast_to(jnp.max(mx_ref[...], axis=-1, keepdims=True), mx_ref.shape)
+    den_ref[...] = jnp.zeros_like(den_ref)
+    acc_ref[...] = jnp.zeros_like(acc_ref)
+
+    def second(j, _):
+        mx = mx_ref[...]
+        p = [jnp.exp2(sc_ref[j, :, i * HEAD:(i + 1) * HEAD] - mx) for i in range(sd // HEAD)]
+        den_ref[...] += functools.reduce(jnp.add, p)
+        vb = v_ref[pl.ds(pl.multiple_of(j * sd, sd), sd), :]
+        acc_ref[...] += jnp.dot(jnp.concatenate([a.astype(BF16) for a in p], axis=-1), vb, preferred_element_type=F32)
+        return 0
+
+    lax.fori_loop(0, ci + 1, second, 0)
+    o = (acc_ref[...] / jnp.sum(den_ref[...], axis=-1, keepdims=True)).astype(BF16)
+    for h in range(per):
+        o_ref[:, h * HEAD:(h + 1) * HEAD] = o[h * sd:(h + 1) * sd, :]
 
 
 def attention(ci, q, kv, c, s, ncp):
@@ -177,7 +186,7 @@
     steps = nh // per
     ga = grp // per
     return pl.pallas_call(
-        functools.partial(attend_kernel, grp),
+        functools.partial(attend_kernel, per),
         grid_spec=pltpu.PrefetchScalarGridSpec(
             num_scalar_prefetch=1,
             grid=(steps,),
@@ -189,7 +198,7 @@
                 pl.BlockSpec((sd, HEAD), lambda i, ci: (0, 0)),
             ],
             out_specs=pl.BlockSpec((sd, per * HEAD), lambda i, ci: (0, i)),
-            scratch_shapes=[pltpu.VMEM((ncp, sd, sd), F32)],
+            scratch_shapes=[pltpu.VMEM((per * sd, HEAD), BF16), pltpu.VMEM((ncp, per * sd, sd), F32)] + [pltpu.VMEM((per * sd, HEAD), F32)] * 3,
         ),
         out_shape=jax.ShapeDtypeStruct((sd, qd), BF16),
         cost_estimate=pl.CostEstimate(flops=16 * sd * kv.shape[0] * qd, bytes_accessed=8 << 20, transcendentals=0),
@@ -197,7 +206,29 @@
     )(ci, q, kv, kv, c, s)
 
 
-def combine_kernel(cap, back_ref, gate_ref, ex_ref, zero_ref, u_ref, y_ref, f_ref, h_ref, acc_ref):
+def hidden_kernel(x_ref, g_ref, w_ref, o_ref):
+    x = x_ref[...]
+    a = jnp.dot(x, g_ref[...], preferred_element_type=F32)
+    o_ref[...] = (a * (1.0 / (1.0 + jnp.exp(-a))) * jnp.dot(x, w_ref[...], preferred_element_type=F32)).astype(BF16)
+
+
+def hidden(x, wg, wu, rows):
+    n, d = x.shape
+    ff = wg.shape[1]
+    return pl.pallas_call(
+        hidden_kernel,
+        grid=(n // rows,),
+        out_shape=jax.ShapeDtypeStruct((n, ff), BF16),
+        in_specs=[pl.BlockSpec((rows, d), lambda i: (i, 0)), pl.BlockSpec((d, ff), lambda i: (0, 0)), pl.BlockSpec((d, ff), lambda i: (0, 0))],
+        out_specs=pl.BlockSpec((rows, ff), lambda i: (i, 0)),
+        cost_estimate=pl.CostEstimate(flops=4 * n * d * ff, bytes_accessed=n * d * 2, transcendentals=0),
+        compiler_params=pltpu.CompilerParams(vmem_limit_bytes=48 << 20),
+        name="hidden",
+    )(x, wg, wu)
+
+
+def combine_kernel(cap, back_ref, gate_ref, ex_ref, zero_ref, u_ref, y_ref, f_ref, *rest):
+    h_ref, acc_ref = rest[-2:]
     rows = back_ref.shape[0]
     t, nexp = ex_ref.shape
     r = pl.program_id(0) * rows + lax.broadcasted_iota(jnp.int32, (nexp, rows), 1)
@@ -224,21 +255,24 @@
         h_ref[...] = (y_ref[...].astype(F32) + f_ref[...].astype(F32) + acc_ref[...]).astype(BF16)
 
 
-def combine(back, gate, ex, zero, u, y, f, cap):
+def combine(back, gate, ex, zero, u, y, f, cap, part, prior):
     t, d = u.shape
     nexp = ex.shape[1]
     rows = 16 * cap
+    cols = back.shape[1]
     whole = lambda a: pl.BlockSpec(a.shape, lambda i: (0, 0))
+    mine = pl.BlockSpec((t, cols), lambda i: (0, part))
     return pl.pallas_call(
         functools.partial(combine_kernel, cap),
         grid=(nexp * cap // rows,),
         out_shape=jax.ShapeDtypeStruct((t, d), BF16),
-        in_specs=[pl.BlockSpec((rows, d), lambda i: (i, 0))] + [whole(a) for a in (gate, ex, zero, u, y, f)],
-        out_specs=pl.BlockSpec((t, d), lambda i: (0, 0)),
-        scratch_shapes=[pltpu.VMEM((t, d), F32)],
-        cost_estimate=pl.CostEstimate(flops=6 * nexp * cap * t * d, bytes_accessed=nexp * cap * d * 2, transcendentals=0),
+        in_specs=[pl.BlockSpec((rows, cols), lambda i: (i, 0))] + [whole(a) for a in (gate, ex, zero)] + [mine] * 3 + [pl.BlockSpec(memory_space=pl.ANY)] * len(prior),
+        out_specs=mine,
+        scratch_shapes=[pltpu.VMEM((t, cols), F32)],
+        input_output_aliases={7: 0} if prior else {},
+        cost_estimate=pl.CostEstimate(flops=6 * nexp * cap * t * cols, bytes_accessed=nexp * cap * cols * 2, transcendentals=0),
         name="combine",
-    )(back, gate, ex, zero, u, y, f)
+    )(back, gate, ex, zero, u, y, f, *prior)
 
 
 def solution(mesh):
@@ -259,21 +293,30 @@
 
         c, s = rope_tables(ci * sd + jnp.arange(sd))
         n, u, kv, gate, zero, ex, ext = front(x, ids, g_attn, g_moe, wk, wv, wr, c, s, ndev)
-        kv = lax.all_gather(kv, 'cp', axis=0, tiled=True)
         send = dispatch(ext, u, cap)
         recv = lax.all_to_all(send, axes, 0, 0, tiled=True)
-
         q = proj(n, wq)
+        recv, kv = lax.optimization_barrier((recv, kv))
+        kv = lax.all_gather(kv, 'cp', axis=0, tiled=True)
+
+        hid = hidden(recv, we_g[0], we_u[0], 16 * cap)
+        wd = we_d[0]
+        cols = d // PARTS
+        back = []
+        for i in range(PARTS):
+            out = proj(hid, wd[:, i * cols:(i + 1) * cols])
+            back.append(lax.all_to_all(out, axes, 0, 0, tiled=True))
+
         o = attention(ci.reshape(1), q, kv, c, s, ncp)
         y = (x.astype(F32) + proj(o, wo).astype(F32)).astype(BF16)
         z = rms_norm(y, g_ffn)
-        hid = (jax.nn.silu(jnp.dot(z, w1, preferred_element_type=F32)) * jnp.dot(z, w3, preferred_element_type=F32)).astype(BF16)
-        f = proj(hid, w2)
-
-        eh = (jax.nn.silu(jnp.dot(recv, we_g[0], preferred_element_type=F32)) * jnp.dot(recv, we_u[0], preferred_element_type=F32)).astype(BF16)
-        out = proj(eh, we_d[0])
-        back = lax.all_to_all(out, axes, 0, 0, tiled=True)
-        h = combine(back, gate, ex, zero, u, y, f, cap)
+        wide = (jax.nn.silu(jnp.dot(z, w1, preferred_element_type=F32)) * jnp.dot(z, w3, preferred_element_type=F32)).astype(BF16)
+        f = proj(wide, w2)
+
+        h = ()
+        for i in range(PARTS):
+            h = (combine(back[i], gate, ex, zero, u, y, f, cap, i, h),)
+        h = h[0]
         return h.reshape(bd, sd, d)
 
     return jax.shard_map(body, mesh=mesh, in_specs=(tok, tok, rep, rep, rep, rep, rep, rep, rep, rep, rep, rep, rep, exs, exs, exs), out_specs=tok, check_vma=False)

time: 490 us -> 453 us (0.924)
  the two profiles are of different devices: /device:TPU:98 before, /device:TPU:18 now
where the time goes in v3:
time: 453 us
  blocking collectives  170 us (38%)
  Pallas kernels  91.3 us (20%)
  matrix products  78.4 us (17%)
  waiting for transfers between devices  71.4 us (16%)
  starting transfers between devices  17.7 us (4%)
  between operations  13.5 us (3%)
  local copies, waits for them, and re-layouts  9.67 us (2%)
    all_to_all x1, blocking collectives, body(): recv = lax.all_to_all(send, axes, 0, 0, tiled=True)  170 us
    all_to_all x2, waiting for transfers between devices, body(): back.append(lax.all_to_all(out, axes, 0, 0, tiled=True))  71.4 us
    dot_general x5, matrix products, proj(): return jnp.dot(a, wt, preferred_element_type=F32).astype(BF16)  64.1 us
    pallas_call x2, Pallas kernels, combine(): pl.pallas_call(functools.partial(combine_kernel, cap), grid=(nexp * cap /...  30.8 us
    pallas_call x1, Pallas kernels, hidden(): pl.pallas_call(hidden_kernel, grid=(n // rows,), out_shape=jax.ShapeDtype...  24.3 us
    pallas_call x1, Pallas kernels, attention(): pl.pallas_call(functools.partial(attend_kernel, per), grid_spec=pltpu.Pre...  21.6 us
    all_to_all x2, starting transfers between devices, body(): back.append(lax.all_to_all(out, axes, 0, 0, tiled=True))  17.7 us
    dot_general x1, matrix products, body(): jnp.dot(z, w1, preferred_element_type=F32)  14.3 us
  transfers between devices with their start and end apart: 3, of which 2 were waited for; matrix products, arithmetic and copies ran while one was open for 17% of the time, Pallas kernels for 14%

profile of v3, /device:TPU:18, one launch (start us, length us, event | category | flops | bytes accessed | tf_op | source)
XLA Modules:
  0.0 452.8 jit_solution(6274625594110126978)
XLA Ops:
  6.7 1.4 copy.22.wr_ref
  8.2 0.8 copy.20
  9.0 0.7 reshape.46.ga_ref
  9.7 0.7 reshape.47.gm_ref
  11.1 1.3 copy-done
  12.4 5.0 %front.1 = (bf16[256,2048]{1,0:T(8,128)(2,1)S(1)}, bf16[256,2048]{1,0:T(8,128)(2,1)S(1)}, bf16[256,1024]{1,0:T(8,128)(2,1)}, bf16[768,128]{1,0:T(8,128)(2,1)S(1)...) custom-call(bf16[256,2048]{1,0:T(8,128)(2,1)S(1)} %bitcast.23, ...), custom_call_target="tpu_custom_call" | custom-call | flops 1275068416 | bytes 8388608 | tf_op jit(solution)/shard_map/front/pallas_call | solution.py:96
  17.4 1.0 copy-done.2
  19.0 1.0 copy-done.7
  22.0 9.5 %dispatch.1 = bf16[3072,2048]{1,0:T(8,128)(2,1)} custom-call(bf16[128,256]{1,0:T(8,128)(2,1)} %copy-done.5, bf16[256,2048]{1,0:T(8,128)(2,1)} %copy-done.2), custom_call_target="tpu_custom_call" | custom-call | flops 3221225472 | bytes 12582912 | tf_op jit(solution)/shard_map/dispatch/pallas_call | solution.py:123
  31.5 170.1 %all_to_all.34 = bf16[128,24,2048]{2,1,0:T(8,128)(2,1)} all-to-all(bf16[128,24,2048]{2,1,0:T(8,128)(2,1)} %bitcast.26), channel_id=1, replica_groups=mesh['dp'=1,'b'=16,'cp'=8] {'b','cp'}, dimensions={0} | all-to-all | bytes 25165824 | tf_op jit(solution)/shard_map/all_to_all | solution.py:297
  201.6 24.3 %hidden.1 = bf16[3072,768]{1,0:T(8,128)(2,1)} custom-call(bf16[3072,2048]{1,0:T(8,128)(2,1)} %bitcast.27, bf16[2048,768]{1,0:T(8,128)(2,1)S(1)} %bitcast.25, bf16[2048,768]{1,0:T(8,128)(2,1)} %bitcast.30), custom_call_target="tpu_custom_call" | custom-call | flops 19327352832 | bytes 12582912 | tf_op jit(solution)/shard_map/hidden/pallas_call | solution.py:218
  225.9 9.4 %convolution_convert_fusion = bf16[3072,1024]{1,0:T(8,128)(2,1)} fusion(bf16[3072,768]{1,0:T(8,128)(2,1)} %hidden.1, bf16[768,2048]{1,0:T(8,128)(2,1)S(1)} %bitcast.31), kind=kOutput, calls=%fused_computation.2 | convolution fusion | flops 4834983936 | bytes 12582912 | tf_op jit(solution)/shard_map/dot_general | solution.py:28
  235.2 11.5 %all-to-all-start.2 = ((bf16[128,24,1024]{2,1,0:T(8,128)(2,1)}), bf16[128,24,1024]{2,1,0:T(8,128)(2,1)}, u32[]{:S(2)}, u32[]{:S(2)}) async-start(bf16[128,24,1024]{2,1,0:T(8,128)(2,1)} %bitcast.29), calls=%async_computation.2 | async-start | bytes 12582912 | tf_op jit(solution)/shard_map/all_to_all | solution.py:308
  246.8 11.7 %convolution_convert_fusion.2.q_ref = bf16[256,4096]{1,0:T(8,128)(2,1)} fusion(bf16[256,2048]{1,0:T(8,128)(2,1)S(1)} %copy-done.8, bf16[2048,4096]{1,0:T(8,128)(2,1)} %param.19), kind=kOutput, calls=%fused_computation.4 | convolution fusion | flops 4296015872 | bytes 19922944 | tf_op jit(solution)/shard_map/dot_general | solution.py:28
  258.5 9.3 %convolution_convert_fusion.1 = bf16[3072,1024]{1,0:T(8,128)(2,1)} fusion(bf16[3072,768]{1,0:T(8,128)(2,1)} %hidden.1, bf16[768,2048]{1,0:T(8,128)(2,1)S(1)} %bitcast.32), kind=kOutput, calls=%fused_computation.3 | convolution fusion | flops 4834983936 | bytes 12582912 | tf_op jit(solution)/shard_map/dot_general | solution.py:28
  267.8 21.6 %attention.1 = bf16[256,4096]{1,0:T(8,128)(2,1)} custom-call(s32[1]{0:T(128)} %bitcast.9.ci_ref, bf16[256,4096]{1,0:T(8,128)(2,1)} %convolution_convert_fusion.2.q_ref, bf16[2048,1024]{1,0:T(8,128)(2,1)} %all-gather.2.cloned.1.call-done.k_ref.v_ref, bf16[2048,1024]{1,0:T(8,128)(2,1)} %all-gather.2.cloned.1.call-done.k_ref.v_ref, f32[256,128]{1,0:T(8,128)} %copy-done.3, ...), custom_call_target="tpu_custom_call" | custom-call | flops 34359738368 | bytes 8388608 | tf_op jit(solution)/shard_map/attention/pallas_call | solution.py:188
  289.5 11.1 %fusion.7 = (f32[256]{0:T(256)S(1)}, bf16[256,2048]{1,0:T(8,128)(2,1)S(1)}) fusion(bf16[256,4096]{1,0:T(8,128)(2,1)} %attention.1, bf16[4096,2048]{1,0:T(8,128)(2,1)} %param.22, bf16[1,256,2048]{2,1,0:T(8,128)(2,1)S(1)} %copy-done.1), kind=kOutput, calls=%fused_computation.14 | convolution fusion | flops 4299161600 | bytes 20972544 | tf_op jit(solution)/shard_map/dot_general | solution.py:28
  300.6 35.0 %all-to-all-done.2 = bf16[128,24,1024]{2,1,0:T(8,128)(2,1)} async-done(((bf16[128,24,1024]{2,1,0:T(8,128)(2,1)}), bf16[128,24,1024]{2,1,0:T(8,128)(2,1)}, u32[]{:S(2)}, u32[]{:S(2)}) %all-to-all-start.2) | async-done | bytes 6291488 | tf_op jit(solution)/shard_map/all_to_all | solution.py:308
  335.5 6.2 %all-to-all-start.1 = ((bf16[128,24,1024]{2,1,0:T(8,128)(2,1)}), bf16[128,24,1024]{2,1,0:T(8,128)(2,1)}, u32[]{:S(2)}, u32[]{:S(2)}) async-start(bf16[128,24,1024]{2,1,0:T(8,128)(2,1)} %bitcast.28), calls=%async_computation.1 | async-start | bytes 12582912 | tf_op jit(solution)/shard_map/all_to_all | solution.py:308
  341.7 14.3 %fusion.14 = f32[256,6144]{1,0:T(8,128)} fusion(bf16[2048,6144]{1,0:T(8,128)(2,1)} %param.24, bf16[256,2048]{1,0:T(8,128)(2,1)S(1)} %get-tuple-element.27.y_ref, f32[2048]{0:T(1024)S(1)} %convert_element_type.51, f32[256]{0:T(256)S(1)} %add_rsqrt_fusion), kind=kOutput, calls=%fused_computation.19 | convolution fusion | flops 6444548096 | bytes 32515072 | tf_op jit(solution)/shard_map/dot_general | solution.py:313
  356.1 22.7 %fusion.6.f_ref = bf16[256,2048]{1,0:T(8,128)(2,1)} fusion(bf16[6144,2048]{1,0:T(8,128)(2,1)} %param.26, bf16[2048,6144]{1,0:T(8,128)(2,1)} %param.25, f32[256,6144]{1,0:T(8,128)} %fusion.14, bf16[256,2048]{1,0:T(8,128)(2,1)S(1)} %get-tuple-element.27.y_ref, f32[2048]{0:T(1024)S(1)} %convert_element_type.51, f32[256]{0:T(256)S(1)} %add_rsqrt_fusion), kind=kOutput, calls=%fused_computation.13 | convolution fusion | flops 12896960512 | bytes 58729472 | tf_op jit(solution)/shard_map/dot_general | solution.py:28
  378.7 15.4 %combine.2.rest_0_ = bf16[256,2048]{1,0:T(8,128)(2,1)} custom-call(bf16[3072,1024]{1,0:T(8,128)(2,1)} %bitcast.11.back_ref, bf16[768,128]{1,0:T(8,128)(2,1)} %copy-done.9, bf16[256,128]{1,0:T(8,128)(2,1)} %copy-done.11, f32[256,128]{1,0:T(8,128)} %copy-done.10, bf16[256,2048]{1,0:T(8,128)(2,1)} %copy-done.2, bf16[256,2048]{1,0:T(8,128)(2,1)} %copy-done.15, ...), custom_call_target="tpu_custom_call" | custom-call | flops 4831838208 | bytes 6291456 | tf_op jit(solution)/shard_map/combine/pallas_call | solution.py:265
  394.1 36.4 %all-to-all-done.1 = bf16[128,24,1024]{2,1,0:T(8,128)(2,1)} async-done(((bf16[128,24,1024]{2,1,0:T(8,128)(2,1)}), bf16[128,24,1024]{2,1,0:T(8,128)(2,1)}, u32[]{:S(2)}, u32[]{:S(2)}) %all-to-all-start.1) | async-done | bytes 6291488 | tf_op jit(solution)/shard_map/all_to_all | solution.py:308
  430.5 15.4 %combine.3 = bf16[256,2048]{1,0:T(8,128)(2,1)} custom-call(bf16[3072,1024]{1,0:T(8,128)(2,1)} %bitcast.8.back_ref, bf16[768,128]{1,0:T(8,128)(2,1)} %copy-done.9, bf16[256,128]{1,0:T(8,128)(2,1)} %copy-done.11, f32[256,128]{1,0:T(8,128)} %copy-done.10, bf16[256,2048]{1,0:T(8,128)(2,1)} %copy-done.2, ...), custom_call_target="tpu_custom_call", output_to_operand_aliasing={{}: (7, {})} | custom-call | flops 4831838208 | bytes 6291456 | tf_op jit(solution)/shard_map/combine/pallas_call | solution.py:265
  (42 shorter events, 3.5 us)
Async XLA Ops:
  6.5 261.3 %all-gather.2.cloned.1.call-start = ((), (), s32[]{:S(2)}) async-start(), calls=%async_computation.3 | async-start | bytes 4718592 | tf_op jit(solution)/shard_map/all_gather | solution.py:300
  11.1 20.4 %copy-start.3 = (f32[256,128]{1,0:T(8,128)}, f32[256,128]{1,0:T(8,128)S(1)}, u32[]{:S(2)}) copy-start(f32[256,128]{1,0:T(8,128)S(1)} %get-tuple-element.28.c_ref) | copy-start | bytes 393220
  11.1 20.4 %copy-start.4 = (f32[256,128]{1,0:T(8,128)}, f32[256,128]{1,0:T(8,128)S(1)}, u32[]{:S(2)}) copy-start(f32[256,128]{1,0:T(8,128)S(1)} %get-tuple-element.29.s_ref) | copy-start | bytes 393220
  11.1 1.3 copy-start
  17.4 1.0 copy-start.2
  18.4 0.6 copy-start.5
  19.0 1.0 copy-start.7
  20.0 0.7 copy-start.9
  20.7 0.7 copy-start.10
  21.3 0.6 copy-start.11
  31.4 170.1 %copy-start.6 = (bf16[1,2048,768]{2,1,0:T(8,128)(2,1)S(1)}, bf16[1,2048,768]{2,1,0:T(8,128)(2,1)}, u32[]{:S(2)}) copy-start(bf16[1,2048,768]{2,1,0:T(8,128)(2,1)} %param.29) | copy-start | bytes 9437188
  201.6 24.3 %copy-start.13 = (bf16[1,768,2048]{2,1,0:T(8,128)(2,1)S(1)}, bf16[1,768,2048]{2,1,0:T(8,128)(2,1)}, u32[]{:S(2)}) copy-start(bf16[1,768,2048]{2,1,0:T(8,128)(2,1)} %param.31) | copy-start | bytes 9437188
  235.2 11.5 %copy-start.8 = (bf16[256,2048]{1,0:T(8,128)(2,1)S(1)}, bf16[256,2048]{1,0:T(8,128)(2,1)}, u32[]{:S(2)}) copy-start(bf16[256,2048]{1,0:T(8,128)(2,1)} %copy-done.7) | copy-start | bytes 3145732
  235.2 100.3 %all-to-all-start.2 = ((bf16[128,24,1024]{2,1,0:T(8,128)(2,1)}), bf16[128,24,1024]{2,1,0:T(8,128)(2,1)}, u32[]{:S(2)}, u32[]{:S(2)}) async-start(bf16[128,24,1024]{2,1,0:T(8,128)(2,1)} %bitcast.29), calls=%async_computation.2 | async-start | bytes 12582912 | tf_op jit(solution)/shard_map/all_to_all | solution.py:308
  246.8 11.7 %copy-start.12 = (bf16[2048]{0:T(1024)(128)(2,1)S(1)}, bf16[2048]{0:T(1024)(128)(2,1)}, u32[]{:S(2)}) copy-start(bf16[2048]{0:T(1024)(128)(2,1)} %param.23) | copy-start | bytes 12292
  246.8 11.7 %copy-start.14 = (bf16[1,768,2048]{2,1,0:T(8,128)(2,1)S(1)}, bf16[1,768,2048]{2,1,0:T(8,128)(2,1)}, u32[]{:S(2)}) copy-start(bf16[1,768,2048]{2,1,0:T(8,128)(2,1)} %param.31) | copy-start | bytes 9437188
  267.8 21.6 %copy-start.1 = (bf16[1,256,2048]{2,1,0:T(8,128)(2,1)S(1)}, bf16[1,256,2048]{2,1,0:T(8,128)(2,1)}, u32[]{:S(2)}) copy-start(bf16[1,256,2048]{2,1,0:T(8,128)(2,1)} %param.16) | copy-start | bytes 3145732
  300.5 55.5 %copy-start.15 = (bf16[256,2048]{1,0:T(8,128)(2,1)}, bf16[256,2048]{1,0:T(8,128)(2,1)S(1)}, u32[]{:S(2)}) copy-start(bf16[256,2048]{1,0:T(8,128)(2,1)S(1)} %get-tuple-element.27.y_ref) | copy-start | bytes 3145732
  335.5 94.9 %all-to-all-start.1 = ((bf16[128,24,1024]{2,1,0:T(8,128)(2,1)}), bf16[128,24,1024]{2,1,0:T(8,128)(2,1)}, u32[]{:S(2)}, u32[]{:S(2)}) async-start(bf16[128,24,1024]{2,1,0:T(8,128)(2,1)} %bitcast.28), calls=%async_computation.1 | async-start | bytes 12582912 | tf_op jit(solution)/shard_map/all_to_all | solution.py:308
Sparse Core Ops, SparseCore 0:
  201.7 33.7 all-gather.1

commit v4 on v3

--- a/solution.py
+++ b/solution.py
@@ -89,22 +89,14 @@
     ext_ref[...] = rank.T.astype(BF16)
 
 
-def front(x, ids, ga, gm, wk, wv, wr, c, s, nexp):
-    t, d = x.shape
-    kd = wk.shape[1]
-    shapes = [((t, d), BF16), ((t, d), BF16), ((t, 2 * kd), BF16), ((3 * t, nexp), BF16), ((t, HEAD), F32), ((t, nexp), BF16), ((nexp, t), BF16)]
-    return pl.pallas_call(
-        front_kernel,
-        out_shape=[jax.ShapeDtypeStruct(*a) for a in shapes],
-        in_specs=vmem(9),
-        out_specs=vmem(7),
-        cost_estimate=pl.CostEstimate(flops=2 * t * d * (2 * kd + wr.shape[1]), bytes_accessed=8 << 20, transcendentals=0),
-        compiler_params=pltpu.CompilerParams(vmem_limit_bytes=48 << 20),
-        name="front",
-    )(x, ids, ga.reshape(1, d), gm.reshape(1, d), wk, wv, wr, c, s)
-
-
-def dispatch_kernel(cap, ext_ref, u_ref, o_ref):
+def front_dispatch_kernel(cap, *refs):
+    *first, o_ref, ext_ref = refs
+
+    @pl.when(pl.program_id(0) == 0)
+    def _():
+        front_kernel(*first, ext_ref)
+
+    u_ref = first[10]
     rows = o_ref.shape[0]
     nexp = ext_ref.shape[0]
     r = pl.program_id(0) * rows + lax.broadcasted_iota(jnp.int32, (rows, nexp), 0)
@@ -116,19 +108,24 @@
     o_ref[...] = jnp.dot(sel, u_ref[...], preferred_element_type=F32).astype(BF16)
 
 
-def dispatch(ext, u, cap):
-    nexp, t = ext.shape
-    d = u.shape[1]
+def front(x, ids, ga, gm, wk, wv, wr, c, s, nexp, cap):
+    t, d = x.shape
+    kd = wk.shape[1]
     rows = 16 * cap
-    return pl.pallas_call(
-        functools.partial(dispatch_kernel, cap),
+    shapes = [((t, d), BF16), ((t, d), BF16), ((t, 2 * kd), BF16), ((3 * t, nexp), BF16), ((t, HEAD), F32), ((t, nexp), BF16)]
+    args = (x, ids, ga.reshape(1, d), gm.reshape(1, d), wk, wv, wr, c, s)
+    whole = lambda sh: pl.BlockSpec(sh, lambda i: (0, 0))
+    return pl.pallas_call(
+        functools.partial(front_dispatch_kernel, cap),
         grid=(nexp * cap // rows,),
-        out_shape=jax.ShapeDtypeStruct((nexp * cap, d), BF16),
-        in_specs=[pl.BlockSpec((nexp, t), lambda i: (0, 0)), pl.BlockSpec((t, d), lambda i: (0, 0))],
-        out_specs=pl.BlockSpec((rows, d), lambda i: (i, 0)),
-        cost_estimate=pl.CostEstimate(flops=2 * nexp * cap * t * d, bytes_accessed=nexp * cap * d * 2, transcendentals=0),
-        name="dispatch",
-    )(ext, u)
+        out_shape=[jax.ShapeDtypeStruct(*a) for a in shapes] + [jax.ShapeDtypeStruct((nexp * cap, d), BF16)],
+        in_specs=[whole(a.shape) for a in args],
+        out_specs=[whole(sh) for sh, _ in shapes] + [pl.BlockSpec((rows, d), lambda i: (i, 0))],
+        scratch_shapes=[pltpu.VMEM((nexp, t), BF16)],
+        cost_estimate=pl.CostEstimate(flops=2 * t * d * (2 * kd + wr.shape[1] + nexp * cap), bytes_accessed=20 << 20, transcendentals=0),
+        compiler_params=pltpu.CompilerParams(vmem_limit_bytes=56 << 20),
+        name="front",
+    )(*args)
 
 
 def attend_kernel(per, ci_ref, q_ref, k_ref, v_ref, c_ref, s_ref, o_ref, q_all, sc_ref, mx_ref, den_ref, acc_ref):
@@ -206,30 +203,58 @@
     )(ci, q, kv, kv, c, s)
 
 
-def hidden_kernel(x_ref, g_ref, w_ref, o_ref):
+def hidden_kernel(ncp, x_ref, g_ref, w_ref, kv_ref, o_ref, all_ref, send_sem, recv_sem):
+    c = lax.axis_index('cp')
+    rows = kv_ref.shape[0]
+
+    def place(p):
+        return all_ref.at[pl.ds(pl.multiple_of(p * rows, rows), rows)]
+
+    def give(p):
+        return pltpu.make_async_remote_copy(
+            src_ref=kv_ref, dst_ref=place(c), send_sem=send_sem.at[p], recv_sem=recv_sem.at[c],
+            device_id={'cp': p}, device_id_type=pl.DeviceIdType.MESH)
+
+    def keep():
+        return pltpu.make_async_copy(kv_ref, place(c), recv_sem.at[c])
+
+    def loop(lo, hi, f):
+        lax.fori_loop(lo, hi, lambda p, _: (f(p), 0)[1], 0)
+
+    @pl.when(pl.program_id(0) == 0)
+    def _():
+        loop(c + 1, ncp, lambda p: give(p).start())
+        keep().start()
+
     x = x_ref[...]
     a = jnp.dot(x, g_ref[...], preferred_element_type=F32)
     o_ref[...] = (a * (1.0 / (1.0 + jnp.exp(-a))) * jnp.dot(x, w_ref[...], preferred_element_type=F32)).astype(BF16)
 
-
-def hidden(x, wg, wu, rows):
+    @pl.when(pl.program_id(0) == pl.num_programs(0) - 1)
+    def _():
+        loop(0, c + 1, lambda p: pltpu.make_async_copy(place(p), place(p), recv_sem.at[p]).wait())
+        loop(c + 1, ncp, lambda p: give(p).wait_send())
+
+
+def hidden(x, wg, wu, kv, rows, ncp):
     n, d = x.shape
     ff = wg.shape[1]
-    return pl.pallas_call(
-        hidden_kernel,
+    hbm = pl.BlockSpec(memory_space=pl.ANY)
+    return pl.pallas_call(
+        functools.partial(hidden_kernel, ncp),
         grid=(n // rows,),
-        out_shape=jax.ShapeDtypeStruct((n, ff), BF16),
-        in_specs=[pl.BlockSpec((rows, d), lambda i: (i, 0)), pl.BlockSpec((d, ff), lambda i: (0, 0)), pl.BlockSpec((d, ff), lambda i: (0, 0))],
-        out_specs=pl.BlockSpec((rows, ff), lambda i: (i, 0)),
+        out_shape=[jax.ShapeDtypeStruct((n, ff), BF16), jax.ShapeDtypeStruct((ncp * kv.shape[0], kv.shape[1]), BF16)],
+        in_specs=[pl.BlockSpec((rows, d), lambda i: (i, 0)), pl.BlockSpec((d, ff), lambda i: (0, 0)), pl.BlockSpec((d, ff), lambda i: (0, 0)), hbm],
+        out_specs=[pl.BlockSpec((rows, ff), lambda i: (i, 0)), hbm],
+        scratch_shapes=[pltpu.SemaphoreType.DMA((ncp,)), pltpu.SemaphoreType.DMA((ncp,))],
         cost_estimate=pl.CostEstimate(flops=4 * n * d * ff, bytes_accessed=n * d * 2, transcendentals=0),
-        compiler_params=pltpu.CompilerParams(vmem_limit_bytes=48 << 20),
+        compiler_params=pltpu.CompilerParams(vmem_limit_bytes=48 << 20, has_side_effects=True),
         name="hidden",
-    )(x, wg, wu)
-
-
-def combine_kernel(cap, back_ref, gate_ref, ex_ref, zero_ref, u_ref, y_ref, f_ref, *rest):
-    h_ref, acc_ref = rest[-2:]
-    rows = back_ref.shape[0]
+    )(x, wg, wu, kv)
+
+
+def weigh_kernel(cap, gate_ref, ex_ref, w_ref):
+    rows = w_ref.shape[1]
     t, nexp = ex_ref.shape
     r = pl.program_id(0) * rows + lax.broadcasted_iota(jnp.int32, (nexp, rows), 1)
     lo = cap * lax.broadcasted_iota(jnp.int32, (nexp, rows), 0)
@@ -237,42 +262,58 @@
     spread = jnp.where(own, 1.0, 0.0).astype(BF16)
     slot = jnp.sum(jnp.where(own, (r - lo).astype(F32), 0.0), axis=0, keepdims=True)
     hit = jnp.dot(ex_ref[...], spread, preferred_element_type=F32) == slot
-    back = back_ref[...]
-
-    @pl.when(pl.program_id(0) == 0)
-    def _():
-        acc_ref[...] = zero_ref[:, :1] * u_ref[...].astype(F32)
-
-    tot = None
     for i in range(3):
         w = jnp.dot(gate_ref[i * t:(i + 1) * t, :], spread, preferred_element_type=F32)
-        p = jnp.dot(jnp.where(hit, w, 0.0).astype(BF16), back, preferred_element_type=F32)
-        tot = p if tot is None else tot + p
-    acc_ref[...] += tot
+        w_ref[i * t:(i + 1) * t, :] = jnp.where(hit, w, 0.0).astype(BF16)
+
+
+def weigh(gate, ex, cap):
+    t3, nexp = gate.shape
+    rows = 16 * cap
+    whole = lambda a: pl.BlockSpec(a.shape, lambda i: (0, 0))
+    return pl.pallas_call(
+        functools.partial(weigh_kernel, cap),
+        grid=(nexp * cap // rows,),
+        out_shape=jax.ShapeDtypeStruct((t3, nexp * cap), BF16),
+        in_specs=[whole(gate), whole(ex)],
+        out_specs=pl.BlockSpec((t3, rows), lambda i: (0, i)),
+        cost_estimate=pl.CostEstimate(flops=3 * t3 * nexp * nexp * cap, bytes_accessed=t3 * nexp * cap * 2, transcendentals=0),
+        name="weigh",
+    )(gate, ex)
+
+
+def combine_kernel(back_ref, w_ref, zero_ref, u_ref, y_ref, f_ref, *rest):
+    h_ref, acc_ref = rest[-2:]
+    t = u_ref.shape[0]
+
+    @pl.when(pl.program_id(0) == 0)
+    def _():
+        acc_ref[...] = zero_ref[:, :1] * u_ref[...].astype(F32)
+
+    p = jnp.dot(w_ref[...], back_ref[...], preferred_element_type=F32)
+    acc_ref[...] += p[:t] + p[t:2 * t] + p[2 * t:]
 
     @pl.when(pl.program_id(0) == pl.num_programs(0) - 1)
     def _():
         h_ref[...] = (y_ref[...].astype(F32) + f_ref[...].astype(F32) + acc_ref[...]).astype(BF16)
 
 
-def combine(back, gate, ex, zero, u, y, f, cap, part, prior):
+def combine(back, w, zero, u, y, f, rows, part, prior):
     t, d = u.shape
-    nexp = ex.shape[1]
-    rows = 16 * cap
-    cols = back.shape[1]
+    n, cols = back.shape
     whole = lambda a: pl.BlockSpec(a.shape, lambda i: (0, 0))
     mine = pl.BlockSpec((t, cols), lambda i: (0, part))
     return pl.pallas_call(
-        functools.partial(combine_kernel, cap),
-        grid=(nexp * cap // rows,),
+        combine_kernel,
+        grid=(n // rows,),
         out_shape=jax.ShapeDtypeStruct((t, d), BF16),
-        in_specs=[pl.BlockSpec((rows, cols), lambda i: (i, 0))] + [whole(a) for a in (gate, ex, zero)] + [mine] * 3 + [pl.BlockSpec(memory_space=pl.ANY)] * len(prior),
+        in_specs=[pl.BlockSpec((rows, cols), lambda i: (i, 0))] + [pl.BlockSpec((3 * t, rows), lambda i: (0, i)), whole(zero)] + [mine] * 3 + [pl.BlockSpec(memory_space=pl.ANY)] * len(prior),
         out_specs=mine,
         scratch_shapes=[pltpu.VMEM((t, cols), F32)],
-        input_output_aliases={7: 0} if prior else {},
-        cost_estimate=pl.CostEstimate(flops=6 * nexp * cap * t * cols, bytes_accessed=nexp * cap * cols * 2, transcendentals=0),
+        input_output_aliases={6: 0} if prior else {},
+        cost_estimate=pl.CostEstimate(flops=6 * n * t * cols, bytes_accessed=n * (cols + 3 * t) * 2, transcendentals=0),
         name="combine",
-    )(back, gate, ex, zero, u, y, f, *prior)
+    )(back, w, zero, u, y, f, *prior)
 
 
 def solution(mesh):
@@ -292,14 +333,11 @@
         ci = lax.axis_index('cp')
 
         c, s = rope_tables(ci * sd + jnp.arange(sd))
-        n, u, kv, gate, zero, ex, ext = front(x, ids, g_attn, g_moe, wk, wv, wr, c, s, ndev)
-        send = dispatch(ext, u, cap)
+        n, u, kv, gate, zero, ex, send = front(x, ids, g_attn, g_moe, wk, wv, wr, c, s, ndev, cap)
         recv = lax.all_to_all(send, axes, 0, 0, tiled=True)
         q = proj(n, wq)
-        recv, kv = lax.optimization_barrier((recv, kv))
-        kv = lax.all_gather(kv, 'cp', axis=0, tiled=True)
-
-        hid = hidden(recv, we_g[0], we_u[0], 16 * cap)
+
+        hid, kv = hidden(recv, we_g[0], we_u[0], kv, 16 * cap, ncp)
         wd = we_d[0]
         cols = d // PARTS
         back = []
@@ -313,9 +351,11 @@
         wide = (jax.nn.silu(jnp.dot(z, w1, preferred_element_type=F32)) * jnp.dot(z, w3, preferred_element_type=F32)).astype(BF16)
         f = proj(wide, w2)
 
+        gate, f = lax.optimization_barrier((gate, f))
+        w = weigh(gate, ex, cap)
         h = ()
         for i in range(PARTS):
-            h = (combine(back[i], gate, ex, zero, u, y, f, cap, i, h),)
+            h = (combine(back[i], w, zero, u, y, f, 16 * cap, i, h),)
         h = h[0]
         return h.reshape(bd, sd, d)
 

time: 453 us -> 469 us (1.035)
  starting transfers between devices: 17.7 us -> 39.7 us
  between operations: 13.5 us -> 0.09 us
  Pallas kernels: 91.3 us -> 103 us
    all_to_all x2, starting transfers between devices: 17.7 us -> 39.7 us  [body(): back.append(lax.all_to_all(out, axes, 0, 0, tiled=True))]
    pallas_call x5, Pallas kernels: 69.6 us -> 81.5 us  [the longest x1 37.1 us: hidden(): pl.pallas_call(functools.partial(hidden_kernel, ncp), grid=(n // rows,),...]
  transfers between devices with their start and end apart: 3 -> 2, of which waited for: 2 -> 2; matrix products, arithmetic and copies ran while one was open for 17% -> 15% of each run, Pallas kernels for 14% -> 9%
where the time goes in v4:
time: 469 us; the launch traced here: 468 us
  blocking collectives  170 us (36%)
  Pallas kernels  103 us (22%)
  matrix products  79.8 us (17%)
  waiting for transfers between devices  67.1 us (14%)
  starting transfers between devices  39.7 us (8%)
  local copies, waits for them, and re-layouts  6.43 us (1%)
    all_to_all x1, blocking collectives, body(): recv = lax.all_to_all(send, axes, 0, 0, tiled=True)  170 us
    all_to_all x2, waiting for transfers between devices, body(): back.append(lax.all_to_all(out, axes, 0, 0, tiled=True))  67.1 us
    dot_general x5, matrix products, proj(): return jnp.dot(a, wt, preferred_element_type=F32).astype(BF16)  65.5 us
    all_to_all x2, starting transfers between devices, body(): back.append(lax.all_to_all(out, axes, 0, 0, tiled=True))  39.7 us
    pallas_call x1, Pallas kernels, hidden(): pl.pallas_call(functools.partial(hidden_kernel, ncp), grid=(n // rows,),...  37.1 us
    pallas_call x2, Pallas kernels, combine(): pl.pallas_call(combine_kernel, grid=(n // rows,), out_shape=jax.ShapeDtyp...  23.9 us
    pallas_call x1, Pallas kernels, attention(): pl.pallas_call(functools.partial(attend_kernel, per), grid_spec=pltpu.Pre...  21.6 us
    dot_general x1, matrix products, body(): jnp.dot(z, w1, preferred_element_type=F32)  14.3 us
  transfers between devices with their start and end apart: 2, of which 2 were waited for; matrix products, arithmetic and copies ran while one was open for 15% of the time, Pallas kernels for 9%

profile of v4, /device:TPU:18, one launch (start us, length us, event | category | flops | bytes accessed | tf_op | source)
XLA Modules:
  0.0 467.6 jit_solution(11142353611870267605)
XLA Ops:
  0.1 0.1 pad.5.clone
  0.2 2.2 copy.22.refs_6_
  2.4 1.5 copy.20
  3.9 1.3 reshape.46.refs_2_
  5.2 1.3 reshape.47.refs_3_
  6.4 0.5 fusion.16
  7.0 0.8 maximum_maximum_fusion
  7.8 14.0 %front.1 = (bf16[256,2048]{1,0:T(8,128)(2,1)}, bf16[256,2048]{1,0:T(8,128)(2,1)}, bf16[256,1024]{1,0:T(8,128)(2,1)}, bf16[768,128]{1,0:T(8,128)(2,1)}, f32[256,1...) custom-call(bf16[256,2048]{1,0:T(8,128)(2,1)} %bitcast.32, s32[256,12]{1,0:T(8,128)} %bitcast.28, ...), custom_call_target="tpu_custom_call" | custom-call | flops 4496293888 | bytes 20971520 | tf_op jit(solution)/shard_map/front/pallas_call | solution.py:118
  21.8 170.1 %all_to_all.33 = bf16[128,24,2048]{2,1,0:T(8,128)(2,1)} all-to-all(bf16[128,24,2048]{2,1,0:T(8,128)(2,1)} %bitcast.24), channel_id=1, replica_groups=mesh['dp'=1,'b'=16,'cp'=8] {'b','cp'}, dimensions={0} | all-to-all | bytes 25165824 | tf_op jit(solution)/shard_map/all_to_all | solution.py:337
  191.9 37.1 %hidden.1 = (bf16[3072,768]{1,0:T(8,128)(2,1)}, bf16[2048,1024]{1,0:T(8,128)(2,1)}) custom-call(bf16[3072,2048]{1,0:T(8,128)(2,1)} %bitcast.25, bf16[2048,768]{1,0:T(8,128)(2,1)S(1)} %bitcast.23, bf16[2048,768]{1,0:T(8,128)(2,1)} %bitcast.29, bf16[256,1024]{1,0:T(8,128)(2,1)S(1)} %copy-done.1), custom_call_target="tpu_custom_call" | custom-call | flops 19327352832 | bytes 12582912 | tf_op jit(solution)/shard_map/hidden/pallas_call | solution.py:243
  229.1 9.4 %convolution_convert_fusion = bf16[3072,1024]{1,0:T(8,128)(2,1)} fusion(bf16[3072,768]{1,0:T(8,128)(2,1)} %get-tuple-element.18, bf16[768,2048]{1,0:T(8,128)(2,1)S(1)} %bitcast.30), kind=kOutput, calls=%fused_computation.2 | convolution fusion | flops 4834983936 | bytes 12582912 | tf_op jit(solution)/shard_map/dot_general | solution.py:28
  238.5 32.7 %all-to-all-start.2 = ((bf16[128,24,1024]{2,1,0:T(8,128)(2,1)}), bf16[128,24,1024]{2,1,0:T(8,128)(2,1)}, u32[]{:S(2)}, u32[]{:S(2)}) async-start(bf16[128,24,1024]{2,1,0:T(8,128)(2,1)} %bitcast.26), calls=%async_computation.2 | async-start | bytes 12582912 | tf_op jit(solution)/shard_map/all_to_all | solution.py:346
  271.2 11.9 %convolution_convert_fusion.2.q_ref = bf16[256,4096]{1,0:T(8,128)(2,1)} fusion(bf16[256,2048]{1,0:T(8,128)(2,1)} %get-tuple-element.20, bf16[2048,4096]{1,0:T(8,128)(2,1)} %param.19), kind=kOutput, calls=%fused_computation.4 | convolution fusion | flops 4296015872 | bytes 19922944 | tf_op jit(solution)/shard_map/dot_general | solution.py:28
  283.2 21.6 %attention.1 = bf16[256,4096]{1,0:T(8,128)(2,1)} custom-call(s32[1]{0:T(128)} %bitcast.9.ci_ref, bf16[256,4096]{1,0:T(8,128)(2,1)} %convolution_convert_fusion.2.q_ref, bf16[2048,1024]{1,0:T(8,128)(2,1)} %get-tuple-element.21.k_ref.v_ref, bf16[2048,1024]{1,0:T(8,128)(2,1)} %get-tuple-element.21.k_ref.v_ref, f32[256,128]{1,0:T(8,128)} %get-tuple-element.32.refs_7_.c_ref, ...), custom_call_target="tpu_custom_call" | custom-call | flops 34359738368 | bytes 8388608 | tf_op jit(solution)/shard_map/attention/pallas_call | solution.py:185
  304.8 12.1 %fusion.7 = (f32[256]{0:T(256)S(1)}, bf16[256,2048]{1,0:T(8,128)(2,1)}) fusion(bf16[256,4096]{1,0:T(8,128)(2,1)} %attention.1, bf16[4096,2048]{1,0:T(8,128)(2,1)} %param.22, bf16[1,256,2048]{2,1,0:T(8,128)(2,1)} %param.16), kind=kOutput, calls=%fused_computation.14 | convolution fusion | flops 4299161600 | bytes 20972544 | tf_op jit(solution)/shard_map/dot_general | solution.py:28
  316.9 9.4 %convolution_convert_fusion.1 = bf16[3072,1024]{1,0:T(8,128)(2,1)} fusion(bf16[3072,768]{1,0:T(8,128)(2,1)} %get-tuple-element.18, bf16[768,2048]{1,0:T(8,128)(2,1)S(1)} %bitcast.31), kind=kOutput, calls=%fused_computation.3 | convolution fusion | flops 4834983936 | bytes 12582912 | tf_op jit(solution)/shard_map/dot_general | solution.py:28
  326.3 33.7 %all-to-all-done.2 = bf16[128,24,1024]{2,1,0:T(8,128)(2,1)} async-done(((bf16[128,24,1024]{2,1,0:T(8,128)(2,1)}), bf16[128,24,1024]{2,1,0:T(8,128)(2,1)}, u32[]{:S(2)}, u32[]{:S(2)}) %all-to-all-start.2) | async-done | bytes 6291488 | tf_op jit(solution)/shard_map/all_to_all | solution.py:346
  360.0 6.9 %all-to-all-start.1 = ((bf16[128,24,1024]{2,1,0:T(8,128)(2,1)}), bf16[128,24,1024]{2,1,0:T(8,128)(2,1)}, u32[]{:S(2)}, u32[]{:S(2)}) async-start(bf16[128,24,1024]{2,1,0:T(8,128)(2,1)} %bitcast.27), calls=%async_computation.1 | async-start | bytes 12582912 | tf_op jit(solution)/shard_map/all_to_all | solution.py:346
  366.9 14.3 %fusion.14 = f32[256,6144]{1,0:T(8,128)} fusion(bf16[2048,6144]{1,0:T(8,128)(2,1)} %param.24, bf16[256,2048]{1,0:T(8,128)(2,1)S(1)} %copy-done.4, f32[2048]{0:T(1024)S(1)} %convert_element_type.51, f32[256]{0:T(256)S(1)} %add_rsqrt_fusion), kind=kOutput, calls=%fused_computation.19 | convolution fusion | flops 6444548096 | bytes 32515072 | tf_op jit(solution)/shard_map/dot_general | solution.py:351
  381.2 22.7 %fusion.6.f_ref = bf16[256,2048]{1,0:T(8,128)(2,1)} fusion(bf16[6144,2048]{1,0:T(8,128)(2,1)} %param.26, bf16[2048,6144]{1,0:T(8,128)(2,1)} %param.25, f32[256,6144]{1,0:T(8,128)} %fusion.14, bf16[256,2048]{1,0:T(8,128)(2,1)S(1)} %copy-done.4, f32[2048]{0:T(1024)S(1)} %convert_element_type.51, f32[256]{0:T(256)S(1)} %add_rsqrt_fusion), kind=kOutput, calls=%fused_computation.13 | convolution fusion | flops 12896960512 | bytes 58729472 | tf_op jit(solution)/shard_map/dot_general | solution.py:28
  403.9 6.4 %weigh.1.w_ref = bf16[768,3072]{1,0:T(8,128)(2,1)} custom-call(bf16[768,128]{1,0:T(8,128)(2,1)} %get-tuple-element.22.gate_ref, bf16[256,128]{1,0:T(8,128)(2,1)} %get-tuple-element.23.ex_ref), custom_call_target="tpu_custom_call" | custom-call | flops 905969664 | bytes 4718592 | tf_op jit(solution)/shard_map/weigh/pallas_call | solution.py:274
  410.3 11.9 %combine.2.rest_0_ = bf16[256,2048]{1,0:T(8,128)(2,1)} custom-call(bf16[3072,1024]{1,0:T(8,128)(2,1)} %bitcast.11.back_ref, bf16[768,3072]{1,0:T(8,128)(2,1)} %weigh.1.w_ref, f32[256,128]{1,0:T(8,128)} %get-tuple-element.24.zero_ref, bf16[256,2048]{1,0:T(8,128)(2,1)} %get-tuple-element.25.u_ref, bf16[256,2048]{1,0:T(8,128)(2,1)} %get-tuple-element.31.y_ref, ...), custom_call_target="tpu_custom_call" | custom-call | flops 4831838208 | bytes 11010048 | tf_op jit(solution)/shard_map/combine/pallas_call | solution.py:306
  422.2 33.4 %all-to-all-done.1 = bf16[128,24,1024]{2,1,0:T(8,128)(2,1)} async-done(((bf16[128,24,1024]{2,1,0:T(8,128)(2,1)}), bf16[128,24,1024]{2,1,0:T(8,128)(2,1)}, u32[]{:S(2)}, u32[]{:S(2)}) %all-to-all-start.1) | async-done | bytes 6291488 | tf_op jit(solution)/shard_map/all_to_all | solution.py:346
  455.6 12.0 %combine.3 = bf16[256,2048]{1,0:T(8,128)(2,1)} custom-call(bf16[3072,1024]{1,0:T(8,128)(2,1)} %bitcast.8.back_ref, bf16[768,3072]{1,0:T(8,128)(2,1)} %weigh.1.w_ref, f32[256,128]{1,0:T(8,128)} %get-tuple-element.24.zero_ref, bf16[256,2048]{1,0:T(8,128)(2,1)} %get-tuple-element.25.u_ref, ...), custom_call_target="tpu_custom_call", output_to_operand_aliasing={{}: (6, {})} | custom-call | flops 4831838208 | bytes 11010048 | tf_op jit(solution)/shard_map/combine/pallas_call | solution.py:306
  (17 shorter events, 0.1 us)
Async XLA Ops:
  21.8 170.1 %copy-start = (bf16[1,2048,768]{2,1,0:T(8,128)(2,1)S(1)}, bf16[1,2048,768]{2,1,0:T(8,128)(2,1)}, u32[]{:S(2)}) copy-start(bf16[1,2048,768]{2,1,0:T(8,128)(2,1)} %param.29) | copy-start | bytes 9437188
  21.8 170.1 %copy-start.1 = (bf16[256,1024]{1,0:T(8,128)(2,1)S(1)}, bf16[256,1024]{1,0:T(8,128)(2,1)}, u32[]{:S(2)}) copy-start(bf16[256,1024]{1,0:T(8,128)(2,1)} %get-tuple-element.17.kv_ref) | copy-start | bytes 1572868
  191.9 37.2 %copy-start.3 = (bf16[1,768,2048]{2,1,0:T(8,128)(2,1)S(1)}, bf16[1,768,2048]{2,1,0:T(8,128)(2,1)}, u32[]{:S(2)}) copy-start(bf16[1,768,2048]{2,1,0:T(8,128)(2,1)} %param.31) | copy-start | bytes 9437188
  238.5 121.5 %all-to-all-start.2 = ((bf16[128,24,1024]{2,1,0:T(8,128)(2,1)}), bf16[128,24,1024]{2,1,0:T(8,128)(2,1)}, u32[]{:S(2)}, u32[]{:S(2)}) async-start(bf16[128,24,1024]{2,1,0:T(8,128)(2,1)} %bitcast.26), calls=%async_computation.2 | async-start | bytes 12582912 | tf_op jit(solution)/shard_map/all_to_all | solution.py:346
  271.2 11.9 %copy-start.2 = (bf16[2048]{0:T(1024)(128)(2,1)S(1)}, bf16[2048]{0:T(1024)(128)(2,1)}, u32[]{:S(2)}) copy-start(bf16[2048]{0:T(1024)(128)(2,1)} %param.23) | copy-start | bytes 12292
  360.0 6.9 %copy-start.4 = (bf16[256,2048]{1,0:T(8,128)(2,1)S(1)}, bf16[256,2048]{1,0:T(8,128)(2,1)}, u32[]{:S(2)}) copy-start(bf16[256,2048]{1,0:T(8,128)(2,1)} %get-tuple-element.31.y_ref) | copy-start | bytes 3145732
  360.0 95.7 %all-to-all-start.1 = ((bf16[128,24,1024]{2,1,0:T(8,128)(2,1)}), bf16[128,24,1024]{2,1,0:T(8,128)(2,1)}, u32[]{:S(2)}, u32[]{:S(2)}) async-start(bf16[128,24,1024]{2,1,0:T(8,128)(2,1)} %bitcast.27), calls=%async_computation.1 | async-start | bytes 12582912 | tf_op jit(solution)/shard_map/all_to_all | solution.py:346
